TPU v7x, 32 devices: a whole 2x2x4 slice. The times are simulated.
32 devices in a mesh: grp: 8 (over y, x, core), loc: 4 (over z).
Axes of the slice: x: 2, y: 2, z: 4, core: 2. Of those that a mesh axis runs over, the one named last changes fastest.
Arguments:
- element_values: float32 [8, 442368], P(None, ('grp', 'loc')), may hold values from -6 to 6
- local_map: int32 [442368], P(('grp', 'loc')), may hold values from 0 to 10647, as said below
- send_node: int32 [32, 3072], P(('grp', 'loc')), may hold values from 0 to 10647, as said below
- send_count: int32 [32, 12], P(('grp', 'loc')), may hold values from 0 to 256, as said below
- recv_slot: int32 [32, 3072], P(('grp', 'loc')), may hold values from 0 to 511, as said below
Outputs:
- summed: float32 [8, 442368], P(None, ('grp', 'loc'))
Inputs may be any that keep to these rules, and one draw needn't show every extreme that they name: `local_map`: each device's block lists the nodes of its elements as points of a grid of 22 x 22 x 22 distinct nodes, elements in some order, the grid points numbered in an arbitrary order of the device's own; every number below 10648 appears in each block. `send_node`: the live slots toward one peer name distinct nodes; slots at or past a pair's count hold arbitrary node numbers. `send_count`: counts are zero toward groups past the ends of grp (no wrap), exactly 256 toward the device itself, and between 64 and 256 toward every other peer. `recv_slot`: the live slots from one sender to one owner name distinct owned nodes.
All inputs are finite; a program needn't handle non-finite values.
Results may differ from a plain program's by a relative error of at most 0.0003.
Values sent between devices are 32-bit elements; how exact they have to be, the bound alone decides.
A program may use at most 64 MiB of HBM per device.

v0:
```python
import jax
import jax.numpy as jnp
from jax import lax
from jax.experimental import pallas as pl
from jax.experimental.pallas import tpu as pltpu
from jax.sharding import PartitionSpec as P

LOCAL = 10648


def shifted(block, axis, distance):
    devices = range(lax.axis_size(axis))
    route = [(i - distance, i) for i in devices if i - distance in devices]
    return lax.ppermute(block, axis, route)


def within_inward(buffer):
    return lax.all_to_all(buffer, "loc", split_axis=2, concat_axis=2, tiled=True)


def across_inward(buffer):
    lower = shifted(buffer[:, 0], "grp", -1)
    upper = shifted(buffer[:, 2], "grp", 1)
    return jnp.stack([lower, buffer[:, 1], upper], axis=1)


def within_outward(buffer):
    return lax.all_to_all(buffer, "loc", split_axis=2, concat_axis=2, tiled=True)


def across_outward(buffer):
    lower = shifted(buffer[:, 0], "grp", 1)
    upper = shifted(buffer[:, 2], "grp", -1)
    return jnp.stack([lower, buffer[:, 1], upper], axis=1)


BATCH = 32
ROWS = 10656


def add_rows(index_ref, value_ref, table_ref):
    def step(b, carry):
        base = pl.multiple_of(b * BATCH, BATCH)
        nodes = [index_ref[base + k] for k in range(BATCH)]
        held = [table_ref[pl.ds(n, 1), :] for n in nodes]
        sums = [held[k] + value_ref[pl.ds(base + k, 1), :] for k in range(BATCH)]
        for k in range(BATCH):
            table_ref[pl.ds(nodes[k], 1), :] = sums[k]
        return carry

    lax.fori_loop(0, index_ref.shape[0] // BATCH, step, 0)


def take_rows(index_ref, table_ref, out_ref):
    def step(b, carry):
        base = pl.multiple_of(b * BATCH, BATCH)
        rows = [table_ref[pl.ds(index_ref[base + k], 1), :] for k in range(BATCH)]
        for k in range(BATCH):
            out_ref[pl.ds(base + k, 1), :] = rows[k]
        return carry

    lax.fori_loop(0, index_ref.shape[0] // BATCH, step, 0)


def assemble_kernel(map_ref, send_ref, value_ref, table_ref, picked_ref):
    chunk = 288

    def clear(b, carry):
        table_ref[pl.ds(pl.multiple_of(b * chunk, chunk), chunk), :] = jnp.zeros((chunk, table_ref.shape[1]), jnp.float32)
        return carry

    lax.fori_loop(0, ROWS // chunk, clear, 0)
    add_rows(map_ref, value_ref, table_ref)
    take_rows(send_ref, table_ref, picked_ref)


def finish_kernel(map_ref, send_ref, change_ref, table_in, out_ref, table_ref):
    pltpu.sync_copy(table_in, table_ref)
    add_rows(send_ref, change_ref, table_ref)
    take_rows(map_ref, table_ref, out_ref)


SMEM = pl.BlockSpec(memory_space=pltpu.SMEM)
VMEM = pl.BlockSpec(memory_space=pltpu.VMEM)


def on_device(element_values, local_map, send_node, send_count, recv_slot):
    fields, span = element_values.shape
    loc_count = lax.axis_size("loc")
    slots_all = send_node.shape[1]
    slot_count = slots_all // (3 * loc_count)
    owned_count = 2 * slot_count
    params = pltpu.CompilerParams(vmem_limit_bytes=48 * 1024 * 1024)
    table, picked_rows = pl.pallas_call(
        assemble_kernel,
        out_shape=(
            jax.ShapeDtypeStruct((ROWS, fields), jnp.float32),
            jax.ShapeDtypeStruct((slots_all, fields), jnp.float32),
        ),
        in_specs=[SMEM, SMEM, VMEM],
        out_specs=(VMEM, VMEM),
        compiler_params=params,
    )(local_map, send_node[0], element_values.T)
    live_slot = (jnp.arange(slot_count)[None, :] < send_count[0][:, None]).reshape(-1)
    picked = jnp.where(live_slot[None, :], picked_rows.T, 0.0)
    outgoing = picked.reshape(fields, 3, loc_count, slot_count)
    arrived = within_inward(across_inward(outgoing))
    incoming = arrived.reshape(fields, -1)
    targets = recv_slot[0]
    totals = jnp.zeros((fields, owned_count), jnp.float32).at[:, targets].add(incoming, mode="promise_in_bounds")
    replies = totals.at[:, targets].get(mode="promise_in_bounds").reshape(fields, 3, loc_count, slot_count)
    homeward = across_outward(within_outward(replies))
    returned = homeward.reshape(fields, -1)
    change = jnp.where(live_slot[None, :], returned - picked, 0.0)
    spots = jnp.where(live_slot, send_node[0], LOCAL)
    summed = pl.pallas_call(
        finish_kernel,
        out_shape=jax.ShapeDtypeStruct((span, fields), jnp.float32),
        in_specs=[SMEM, SMEM, VMEM, pl.BlockSpec(memory_space=pl.ANY)],
        out_specs=VMEM,
        scratch_shapes=[pltpu.VMEM((ROWS, fields), jnp.float32)],
        compiler_params=params,
    )(local_map, spots, change.T, table)
    return summed.T


def solution(mesh):
    return jax.shard_map(
        on_device,
        mesh=mesh,
        in_specs=(
            P(None, ("grp", "loc")),
            P(("grp", "loc")),
            P(("grp", "loc"), None),
            P(("grp", "loc"), None),
            P(("grp", "loc"), None),
        ),
        out_specs=P(None, ("grp", "loc")),
        check_vma=False,
    )
```

profile of v0, /device:TPU:1, one launch (start us, length us, event | category | flops | bytes accessed | tf_op | source)
XLA Modules:
  0.0 139.7 jit_solution(14062402565776738454)
XLA Ops:
  0.0 0.0 copy-start.3
  0.0 0.0 copy-start.1
  0.0 0.0 copy-start
  0.0 5.1 %copy.30 = f32[8,13824]{0,1:T(8,128)} copy(f32[8,13824]{1,0:T(8,128)} %param.5) | data formatting | bytes 884736 | tf_op args[0]
  5.2 0.0 copy-done.3
  5.2 0.1 iota_compare_fusion
  5.3 0.0 copy-done.1
  5.3 0.0 copy-done
  5.3 36.0 %shard_map.55 = (f32[10656,8]{1,0:T(8,128)}, f32[3072,8]{1,0:T(8,128)S(1)}) custom-call(s32[13824]{0:T(1024)S(1)} %copy-done, s32[3072]{0:T(1024)S(1)} %bitcast.35, f32[13824,8]{1,0:T(8,128)} %bitcast.37), custom_call_target="tpu_custom_call" | custom-call | tf_op jit(solution)/shard_map/pallas_call | solution.py:94
  41.3 1.6 %broadcast_select_fusion = f32[3072,8]{1,0:T(8,128)S(1)} fusion(f32[3072,8]{1,0:T(8,128)S(1)} %get-tuple-element.7, pred[3072]{0:T(1024)(128)(4,1)S(1)} %lt.38), kind=kLoop, calls=%fused_computation.4 | loop fusion | flops 24576 | bytes 199680 | tf_op jit(solution)/shard_map/jit(_where)/select_n | solution.py:105
  42.9 0.0 copy-start.2
  42.9 0.1 fusion.3
  43.0 0.2 copy.44
  43.1 4.5 %collective-permute-start.1 = (f32[8,4,256]{2,0,1:T(8,128)S(1)}, f32[8,4,256]{2,0,1:T(8,128)S(1)}, u32[]{:S(2)}, u32[]{:S(2)}) collective-permute-start(f32[8,4,256]{2,0,1:T(8,128)S(1)} %bitcast.44), channel_id=1, source_target_pairs={{0,4},{4,8},{8,12},{12,16},{16,20},{20,24},{24,28},{1,5},{5,9},{9,... | collective-permute-start | bytes 98312 | tf_op jit(solution)/shard_map/ppermute | solution.py:14
  47.6 0.2 copy.42
  47.8 1.9 %collective-permute-start = (f32[8,4,256]{2,0,1:T(8,128)S(1)}, f32[8,4,256]{2,0,1:T(8,128)S(1)}, u32[]{:S(2)}, u32[]{:S(2)}) collective-permute-start(f32[8,4,256]{2,0,1:T(8,128)S(1)} %bitcast.45), channel_id=1, source_target_pairs={{4,0},{8,4},{12,8},{16,12},{20,16},{24,20},{28,24},{5,1},{9,5},{13... | collective-permute-start | bytes 98312 | tf_op jit(solution)/shard_map/ppermute | solution.py:14
  49.7 0.0 copy-done.2
  49.8 0.2 copy.43
  49.9 0.0 collective-permute-done.1
  49.9 3.1 %collective-permute-done = f32[8,4,256]{2,0,1:T(8,128)S(1)} collective-permute-done((f32[8,4,256]{2,0,1:T(8,128)S(1)}, f32[8,4,256]{2,0,1:T(8,128)S(1)}, u32[]{:S(2)}, u32[]{:S(2)}) %collective-permute-start) | collective-permute-done | bytes 32800 | tf_op jit(solution)/shard_map/ppermute | solution.py:14
  53.0 0.6 copy.34
  53.7 4.6 %all-to-all-start = ((f32[8,3,4,256]{3,0,1,2:T(8,128)}), f32[8,3,4,256]{3,0,1,2:T(8,128)S(1)}, u32[]{:S(2)}, u32[]{:S(2)}) async-start(f32[8,3,4,256]{3,0,1,2:T(8,128)} %copy.34), calls=%async_computation | async-start | bytes 196608 | tf_op jit(solution)/shard_map/all_to_all | solution.py:18
  58.3 4.7 %all-to-all-done = f32[8,3,4,256]{3,0,1,2:T(8,128)S(1)} async-done(((f32[8,3,4,256]{3,0,1,2:T(8,128)}), f32[8,3,4,256]{3,0,1,2:T(8,128)S(1)}, u32[]{:S(2)}, u32[]{:S(2)}) %all-to-all-start) | async-done | bytes 98336 | tf_op jit(solution)/shard_map/all_to_all | solution.py:18
  63.0 0.1 reshape.71
  63.1 0.5 copy.36
  63.5 17.0 %scatter_custom_fusion = f32[8,512]{0,1:T(8,128)S(1)} fusion(s32[3072]{0:T(1024)S(1)} %bitcast.43, f32[3072,8]{1,0:T(8,128)S(1)} %copy.36, f32[]{:T(128)} %constant.0.clone.1), kind=kCustom, calls=%fused_computation.5 | custom fusion | flops 24576 | bytes 16388 | tf_op jit(solution)/shard_map/scatter-add | solution.py:110
  80.5 8.1 %gather_fusion = f32[3072,8]{1,0:T(8,128)S(1)} fusion(f32[8,512]{0,1:T(8,128)S(1)} %scatter_custom_fusion, s32[3072]{0:T(1024)S(1)} %broadcast_clamp_fusion), kind=kCustom, calls=%fused_computation | custom fusion | bytes 208896 | tf_op jit(solution)/shard_map/gather | solution.py:111
  88.6 0.4 copy.37
  89.1 7.3 %all_to_all.10 = f32[8,3,4,256]{3,0,1,2:T(8,128)S(1)} all-to-all(f32[8,3,4,256]{3,0,1,2:T(8,128)S(1)} %copy.37), channel_id=1, replica_groups=mesh['grp'=8,'loc'=4] {'loc'}, dimensions={2} | all-to-all | bytes 196608 | tf_op jit(solution)/shard_map/all_to_all | solution.py:28
  96.4 4.5 %collective-permute-start.2 = (f32[8,4,256]{2,0,1:T(8,128)S(1)}, f32[8,4,256]{2,0,1:T(8,128)S(1)}, u32[]{:S(2)}, u32[]{:S(2)}) collective-permute-start(f32[8,4,256]{2,0,1:T(8,128)S(1)} %get-tuple-element.12), channel_id=1, source_target_pairs={{0,4},{4,8},{8,12},{12,16},{16,20},{20,24},{24,28},{1,5},{5,9},{9,... | collective-permute-start | bytes 98312 | tf_op jit(solution)/shard_map/ppermute | solution.py:14
  100.9 1.9 %collective-permute-start.3 = (f32[8,4,256]{2,0,1:T(8,128)S(1)}, f32[8,4,256]{2,0,1:T(8,128)S(1)}, u32[]{:S(2)}, u32[]{:S(2)}) collective-permute-start(f32[8,4,256]{2,0,1:T(8,128)S(1)} %get-tuple-element.13), channel_id=1, source_target_pairs={{4,0},{8,4},{12,8},{16,12},{20,16},{24,20},{28,24},{5,1},{9,5},{13... | collective-permute-start | bytes 98312 | tf_op jit(solution)/shard_map/ppermute | solution.py:14
  102.9 0.0 collective-permute-done.2
  102.9 3.3 %collective-permute-done.3 = f32[8,4,256]{2,0,1:T(8,128)S(1)} collective-permute-done((f32[8,4,256]{2,0,1:T(8,128)S(1)}, f32[8,4,256]{2,0,1:T(8,128)S(1)}, u32[]{:S(2)}, u32[]{:S(2)}) %collective-permute-start.3) | collective-permute-done | bytes 32800 | tf_op jit(solution)/shard_map/ppermute | solution.py:14
  106.2 0.5 copy.40
  106.6 2.0 %fusion = f32[8,3072]{0,1:T(8,128)S(1)} fusion(f32[8,3,4,256]{0,3,2,1:T(8,128)S(1)} %copy.40, pred[3072]{0:T(1024)(128)(4,1)S(1)} %lt.38, f32[3072,8]{1,0:T(8,128)S(1)} %get-tuple-element.7), kind=kLoop, calls=%fused_computation.3 | loop fusion | flops 73728 | bytes 297984 | tf_op jit(solution)/shard_map/jit(_where)/select_n | solution.py:114
  108.6 25.7 %shard_map.56 = f32[13824,8]{1,0:T(8,128)} custom-call(s32[13824]{0:T(1024)S(1)} %copy-done, s32[3072]{0:T(1024)S(1)} %broadcast_select_fusion.1.send_ref, f32[3072,8]{1,0:T(8,128)S(1)} %bitcast.34, f32[10656,8]{1,0:T(8,128)} %get-tuple-element.8.table_in), custom_call_target="tpu_custom_call" | custom-call | tf_op jit(solution)/shard_map/pallas_call | solution.py:116
  134.3 5.4 %copy.41 = f32[8,13824]{1,0:T(8,128)} copy(f32[8,13824]{0,1:T(8,128)} %bitcast.38) | data formatting | bytes 884736 | tf_op jit(solution)/shard_map/transpose | solution.py:124
  (8 shorter events, 0.1 us)
Async XLA Ops:
  0.0 5.2 %copy-start.3 = (s32[1,12]{1,0:T(1,128)S(1)}, s32[1,12]{1,0:T(1,128)}, u32[]{:S(2)}) copy-start(s32[1,12]{1,0:T(1,128)} %param.8) | copy-start | bytes 148
  0.0 5.3 %copy-start.1 = (s32[1,3072]{1,0:T(1,128)S(1)}, s32[1,3072]{1,0:T(1,128)}, u32[]{:S(2)}) copy-start(s32[1,3072]{1,0:T(1,128)} %param.7) | copy-start | bytes 36868
  0.0 5.3 %copy-start = (s32[13824]{0:T(1024)S(1)}, s32[13824]{0:T(1024)}, u32[]{:S(2)}) copy-start(s32[13824]{0:T(1024)} %map_ref.3) | copy-start | bytes 165892
  42.9 6.9 %copy-start.2 = (s32[1,3072]{1,0:T(1,128)S(1)}, s32[1,3072]{1,0:T(1,128)}, u32[]{:S(2)}) copy-start(s32[1,3072]{1,0:T(1,128)} %param.9) | copy-start | bytes 36868
  43.1 6.8 %collective-permute-start.1 = (f32[8,4,256]{2,0,1:T(8,128)S(1)}, f32[8,4,256]{2,0,1:T(8,128)S(1)}, u32[]{:S(2)}, u32[]{:S(2)}) collective-permute-start(f32[8,4,256]{2,0,1:T(8,128)S(1)} %bitcast.44), channel_id=1, source_target_pairs={{0,4},{4,8},{8,12},{12,16},{16,20},{20,24},{24,28},{1,5},{5,9},{9,... | collective-permute-start | bytes 98312 | tf_op jit(solution)/shard_map/ppermute | solution.py:14
  47.8 5.2 %collective-permute-start = (f32[8,4,256]{2,0,1:T(8,128)S(1)}, f32[8,4,256]{2,0,1:T(8,128)S(1)}, u32[]{:S(2)}, u32[]{:S(2)}) collective-permute-start(f32[8,4,256]{2,0,1:T(8,128)S(1)} %bitcast.45), channel_id=1, source_target_pairs={{4,0},{8,4},{12,8},{16,12},{20,16},{24,20},{28,24},{5,1},{9,5},{13... | collective-permute-start | bytes 98312 | tf_op jit(solution)/shard_map/ppermute | solution.py:14
  53.7 9.3 %all-to-all-start = ((f32[8,3,4,256]{3,0,1,2:T(8,128)}), f32[8,3,4,256]{3,0,1,2:T(8,128)S(1)}, u32[]{:S(2)}, u32[]{:S(2)}) async-start(f32[8,3,4,256]{3,0,1,2:T(8,128)} %copy.34), calls=%async_computation | async-start | bytes 196608 | tf_op jit(solution)/shard_map/all_to_all | solution.py:18
  96.4 6.4 %collective-permute-start.2 = (f32[8,4,256]{2,0,1:T(8,128)S(1)}, f32[8,4,256]{2,0,1:T(8,128)S(1)}, u32[]{:S(2)}, u32[]{:S(2)}) collective-permute-start(f32[8,4,256]{2,0,1:T(8,128)S(1)} %get-tuple-element.12), channel_id=1, source_target_pairs={{0,4},{4,8},{8,12},{12,16},{16,20},{20,24},{24,28},{1,5},{5,9},{9,... | collective-permute-start | bytes 98312 | tf_op jit(solution)/shard_map/ppermute | solution.py:14
  100.9 5.2 %collective-permute-start.3 = (f32[8,4,256]{2,0,1:T(8,128)S(1)}, f32[8,4,256]{2,0,1:T(8,128)S(1)}, u32[]{:S(2)}, u32[]{:S(2)}) collective-permute-start(f32[8,4,256]{2,0,1:T(8,128)S(1)} %get-tuple-element.13), channel_id=1, source_target_pairs={{4,0},{8,4},{12,8},{16,12},{20,16},{24,20},{28,24},{5,1},{9,5},{13... | collective-permute-start | bytes 98312 | tf_op jit(solution)/shard_map/ppermute | solution.py:14
where the time goes:
time: 141 us; the launch traced here: 140 us
  Pallas kernels  61.8 us (44%)
  local copies, waits for them, and re-layouts  21.4 us (15%)
  other arithmetic  20.6 us (15%)
  starting transfers between devices  17.4 us (12%)
  waiting for transfers between devices  11.1 us (8%)
  blocking collectives  7.32 us (5%)
    pallas_call x1, Pallas kernels, on_device(): pl.pallas_call(assemble_kernel, out_shape=(jax.ShapeDtypeStruct((ROWS, fi...  36 us
    pallas_call x1, Pallas kernels, on_device(): pl.pallas_call(finish_kernel, out_shape=jax.ShapeDtypeStruct((span, field...  25.7 us
    scatter-add x1, other arithmetic, on_device(): jnp.zeros((fields, owned_count), jnp.float32).at[:, targets]  17 us
    ppermute x4, starting transfers between devices, shifted(): return lax.ppermute(block, axis, route)  12.8 us
    gather x1, local copies, waits for them, and re-layouts, on_device(): totals.at[:, targets].get(mode='promise_in_bounds')  8.11 us
    all_to_all x1, blocking collectives, within_outward(): lax.all_to_all(buffer, 'loc', split_axis=2, concat_axis=2, tiled=True)  7.32 us
    ppermute x4, waiting for transfers between devices, shifted(): return lax.ppermute(block, axis, route)  6.4 us
    unnamed x12, local copies, waits for them, and re-layouts  5.65 us
  transfers between devices with their start and end apart: 5, of which 3 were waited for; matrix products, arithmetic and copies ran while one was open for 0% of the time, Pallas kernels for 0%

commit v1 on v0

v1 whole, which is shorter than its diff:
```python
import functools

import jax
import jax.numpy as jnp
from jax import lax
from jax.experimental import pallas as pl
from jax.experimental.pallas import tpu as pltpu
from jax.sharding import PartitionSpec as P

MESH = pl.DeviceIdType.MESH
F32, BF16, I32 = jnp.float32, jnp.bfloat16, jnp.int32
SIDE = 8
NODES = SIDE**3
ROWS = NODES // 128
PAIR = 256
BATCH = 32


def blocks_along(span):
    edge = round((span // NODES) ** (1 / 3))
    assert edge**3 * NODES == span and 1 < edge <= 3
    return edge


def iota(shape, axis):
    return lax.broadcasted_iota(I32, shape, axis)


def halves(x):
    high = x.astype(BF16)
    low = (x - high.astype(F32)).astype(BF16)
    return jnp.concatenate([high, low], axis=0)


def add_rows(index_ref, value_ref, table_ref):
    def step(b, carry):
        base = pl.multiple_of(b * BATCH, BATCH)
        nodes = [index_ref[base + k] for k in range(BATCH)]
        held = [table_ref[pl.ds(n, 1), :] for n in nodes]
        sums = [held[k] + value_ref[pl.ds(base + k, 1), :] for k in range(BATCH)]
        for k in range(BATCH):
            table_ref[pl.ds(nodes[k], 1), :] = sums[k]
        return carry

    lax.fori_loop(0, index_ref.shape[0] // BATCH, step, 0)


def take_rows(index_ref, table_ref, out_ref):
    def step(b, carry):
        base = pl.multiple_of(b * BATCH, BATCH)
        rows = [table_ref[pl.ds(index_ref[base + k], 1), :] for k in range(BATCH)]
        for k in range(BATCH):
            out_ref[pl.ds(base + k, 1), :] = rows[k]
        return carry

    lax.fori_loop(0, index_ref.shape[0] // BATCH, step, 0)


def to_rows(flat_ref, rows_ref):
    def step(t, carry):
        base = pl.multiple_of(t * 128, 128)
        block = flat_ref[:, pl.ds(base, 128)]
        wide = jnp.concatenate([block] * (128 // block.shape[0]), axis=0)
        rows_ref[pl.ds(base, 128), :] = wide.T
        return carry

    lax.fori_loop(0, flat_ref.shape[1] // 128, step, 0)


def from_rows(rows_ref, flat_ref, put):
    def step(t, carry):
        base = pl.multiple_of(t * 128, 128)
        put(base, rows_ref[pl.ds(base, 128), :].T[: flat_ref.shape[0]])
        return carry

    lax.fori_loop(0, flat_ref.shape[1] // 128, step, 0)


def general_table(map_hbm, value_ref, map_smem, rows_ref, table_ref):
    pltpu.sync_copy(map_hbm, map_smem)
    chunk = 96

    def clear(b, carry):
        base = pl.multiple_of(b * chunk, chunk)
        table_ref[pl.ds(base, chunk), :] = jnp.zeros((chunk, 128), F32)
        return carry

    lax.fori_loop(0, table_ref.shape[0] // chunk, clear, 0)
    to_rows(value_ref, rows_ref)
    add_rows(map_smem, rows_ref, table_ref)


def sweep(ref, edge):
    lane = iota((ref.shape[0], 128), 1)
    zero = jnp.zeros((ref.shape[0], 128), F32)

    def at(px, py, pz, row):
        return pl.ds((((px * edge + py) * edge + pz) * ROWS + row) * 128, 128)

    def line(spots_of, first, last, shift):
        held = [ref[:, s] for s in spots_of]
        for i, s in enumerate(spots_of):
            total = held[i]
            if i + 1 < edge:
                total = total + jnp.where(last, pltpu.roll(held[i + 1], shift, 1), zero)
            if i > 0:
                total = total + jnp.where(first, pltpu.roll(held[i - 1], 128 - shift, 1), zero)
            ref[:, s] = total

    for py in range(edge):
        for pz in range(edge):
            for px in range(edge - 1):
                a, b = at(px, py, pz, ROWS - 1), at(px + 1, py, pz, 0)
                upper, lower = ref[:, a], ref[:, b]
                ref[:, a] = upper + jnp.where(lane >= 64, pltpu.roll(lower, 64, 1), zero)
                ref[:, b] = lower + jnp.where(lane < 64, pltpu.roll(upper, 64, 1), zero)
    y, z = (lane // SIDE) % SIDE, lane % SIDE
    for px in range(edge):
        for pz in range(edge):
            for row in range(ROWS):
                line([at(px, py, pz, row) for py in range(edge)], y == 0, y == SIDE - 1, SIDE * (SIDE - 1))
    for px in range(edge):
        for py in range(edge):
            for row in range(ROWS):
                line([at(px, py, pz, row) for pz in range(edge)], z == 0, z == SIDE - 1, SIDE - 1)


def find_places(lab_ref, edge):
    count = edge**3
    near, mid, far = (lab_ref[pl.ds(k, 32, stride=ROWS), :].astype(F32) for k in (0, 1, ROWS - 1))
    near_t, mid_t, far_t = near.T, mid.T, far.T
    real = (iota((32, 32), 0) < count) & (iota((32, 32), 1) < count)
    sides = (
        (near, near_t, 27, far, far_t, 91),
        (mid, mid_t, 67, mid, mid_t, 123),
        (mid, mid_t, 88, mid, mid_t, 95),
    )
    place = jnp.zeros((32, 1), F32)
    for low, low_t, i, high, high_t, j in sides:
        before = jnp.where(real & (low[:, i : i + 1] == high_t[j : j + 1, :]), 1.0, 0.0)
        before_t = jnp.where(real & (high[:, j : j + 1] == low_t[i : i + 1, :]), 1.0, 0.0)
        steps = jnp.zeros((1, 32), F32)
        if edge > 2:
            steps = jnp.sum(before_t, axis=0, keepdims=True)
        place = place * edge + jnp.sum(before * (1.0 + steps), axis=1, keepdims=True)
    hit = (iota((32, 32), 0) < count) & (place == iota((32, 32), 1).astype(F32))
    who = jnp.sum(jnp.where(hit, iota((32, 32), 0).astype(F32), 0.0), axis=0, keepdims=True)
    times = jnp.sum(jnp.where(hit, 1.0, 0.0), axis=0, keepdims=True)
    wrong = jnp.where((iota((1, 32), 1) < count) & (times != 1.0), 1, 0)
    return jnp.clip(who.astype(I32), 0, count - 1), wrong


def count_mismatches(grid_ref, edge):
    total = jnp.zeros((1, 128), I32)

    def compare(step, low_row, high_row, low_lane, shift, axis):
        length = edge**3 * ROWS - step + (high_row - low_row if axis == 0 else 0)
        rows = edge**3 * ROWS - step * ROWS
        return length, rows

    strides = (edge * edge, edge, 1)
    lane = iota((1, 128), 1)
    y, z = (lane // SIDE) % SIDE, lane % SIDE
    for axis, stride in enumerate(strides):
        rows = (edge**3 - stride) * ROWS
        gap = stride * ROWS
        low = grid_ref[0:rows, :]
        high = grid_ref[gap : gap + rows, :]
        element = iota((rows, 1), 0) // ROWS
        inner = (element // stride) % edge < edge - 1
        if axis == 0:
            low = grid_ref[0 : rows, :]
            high = grid_ref[gap - (ROWS - 1) : gap - (ROWS - 1) + rows, :]
            where = inner & (iota((rows, 1), 0) % ROWS == ROWS - 1) & (lane < 64)
            shift = 64
        elif axis == 1:
            where, shift = inner & (y == 0), 128 - SIDE * (SIDE - 1)
            shift = 128 - SIDE * (SIDE - 1)
        else:
            where, shift = inner & (z == 0), 128 - (SIDE - 1)
        differ = where & (pltpu.roll(low, shift, 1) != high)
        total = total + jnp.sum(jnp.where(differ, 1, 0), axis=0, keepdims=True)
    return total


def assemble_kernel(
    edge, slot_count, value_ref, map_ref, node_ref, count_ref, map_hbm, node_hbm,
    picked_ref, grid_ref, spot_ref, meta_ref,
    lab_ref, order_ref, a_ref, b_ref, u_ref, map_smem, node_smem, rows_ref, table_ref,
):
    count = edge**3
    lines = map_ref.shape[0]
    slots_all = picked_ref.shape[1]
    slot_rows = node_ref.shape[0]
    local = ((SIDE - 1) * edge + 1) ** 3
    tall = (local + 127) // 128
    tall16 = a_ref.shape[0] // 2

    lab_ref[0:lines, :] = map_ref[...]
    lab_ref[lines:, :] = jnp.zeros((lab_ref.shape[0] - lines, 128), I32)
    who, wrong = find_places(lab_ref, edge)
    for s in range(count):
        e = who[0, s]
        meta_ref[s] = e
        grid_ref[:, s * NODES : (s + 1) * NODES] = value_ref[:, pl.ds(pl.multiple_of(e * NODES, NODES), NODES)]
        for r in range(ROWS):
            order_ref[s * ROWS + r : s * ROWS + r + 1, :] = lab_ref[pl.ds(e * ROWS + r, 1), :]

    lane = iota((1, 128), 1)
    first = (lane >= 64, (lane // SIDE) % SIDE > 0, lane % SIDE > 0)
    high_of = iota((tall16, 128), 0).astype(BF16)
    low_of = iota((128, 128), 0).astype(BF16)
    zero = jnp.bfloat16(0)
    for r in range(lines):
        s = r // ROWS
        place = (s // (edge * edge), (s // edge) % edge, s % edge)
        label = order_ref[r : r + 1, :]
        for axis in range(3):
            if place[axis] > 0 and (axis > 0 or r % ROWS == 0):
                label = jnp.where(first[axis], label, -1)
        high = jnp.broadcast_to((label >> 7).astype(BF16), (tall16, 128))
        low = jnp.broadcast_to((label & 127).astype(BF16), (128, 128))
        col = slice(r * 128, (r + 1) * 128)
        within = jnp.broadcast_to((lane + (r % 2) * 128).astype(BF16), (tall16, 128))
        hit = high == high_of
        a_ref[0:tall16, col] = jnp.where(hit, jnp.bfloat16(r // 2), zero)
        a_ref[tall16:, col] = jnp.where(hit, within, zero)
        b_ref[:, col] = jnp.where(low == low_of, jnp.bfloat16(1), zero)
    found = lax.dot_general(a_ref[...], b_ref[...], (((1,), (1,)), ((), ())), preferred_element_type=F32)
    where_is = found[0:tall16] * PAIR + found[tall16:]

    sweep(grid_ref, edge)
    for r in range(lines // 2):
        u_ref[r * 16 : (r + 1) * 16, :] = halves(grid_ref[:, r * PAIR : (r + 1) * PAIR])

    node = node_ref[...]
    high, low = node >> 7, node & 127
    spot = jnp.zeros((slot_rows, 128), F32)
    for h in range(tall):
        row = jnp.broadcast_to(where_is[h : h + 1, :], (slot_rows, 128))
        spot = jnp.where(high == h, jnp.take_along_axis(row, low, axis=1), spot)
    per = slot_count // 128
    row_of = iota((slot_rows, 128), 0)
    limit = jnp.zeros((slot_rows, 128), I32)
    for p in range(slot_rows // per):
        limit = jnp.where(row_of // per == p, count_ref[p], limit)
    live = (row_of % per) * 128 + iota((slot_rows, 128), 1) < limit
    spot_ref[...] = jnp.where(live, spot.astype(I32), -PAIR)

    within_of = iota((PAIR, PAIR), 0).astype(BF16)

    def pick(n, carry):
        spots = jnp.concatenate([spot_ref[pl.ds(2 * n, 1), :], spot_ref[pl.ds(2 * n + 1, 1), :]], axis=1)
        low = jnp.broadcast_to((spots & (PAIR - 1)).astype(BF16), (PAIR, PAIR))
        onehot = jnp.where(low == within_of, jnp.bfloat16(1), zero)
        both = jnp.dot(u_ref[...], onehot, preferred_element_type=F32)
        which = jnp.broadcast_to(spots >> 8, (8, PAIR))
        top = jnp.zeros((8, PAIR), F32)
        low_part = jnp.zeros((8, PAIR), F32)
        for r in range(lines // 2):
            mine = which == r
            top = jnp.where(mine, both[r * 16 : r * 16 + 8], top)
            low_part = jnp.where(mine, both[r * 16 + 8 : r * 16 + 16], low_part)
        picked_ref[:, pl.ds(pl.multiple_of(n * PAIR, PAIR), PAIR)] = top + low_part
        return carry

    lax.fori_loop(0, slots_all // PAIR, pick, 0)

    bad = jnp.sum(count_mismatches(order_ref, edge)) + jnp.sum(wrong)
    meta_ref[31] = bad

    @pl.when(bad > 0)
    def _():
        general_table(map_hbm, value_ref, map_smem, rows_ref, table_ref)
        pltpu.sync_copy(node_hbm, node_smem)
        take_rows(node_smem, table_ref, rows_ref)

        def put(base, block):
            p = base // slot_count
            keep = base - p * slot_count + iota((8, 128), 1) < count_ref[p]
            picked_ref[:, pl.ds(base, 128)] = jnp.where(keep, block, 0.0)

        from_rows(rows_ref, picked_ref, put)


def finish_kernel(
    edge, slot_count, change_ref, spot_ref, grid_ref, meta_ref, count_ref, value_hbm, map_hbm, node_hbm,
    out_ref,
    delta_ref, a_ref, b_ref, map_smem, node_smem, rows_ref, table_ref,
):
    count = edge**3
    slots_all = change_ref.shape[1]
    blocks = delta_ref.shape[1] // PAIR
    zero = jnp.bfloat16(0)
    within_of = iota((PAIR, 128), 0).astype(BF16)
    for q in range(slots_all // 128):
        col = slice(q * 128, (q + 1) * 128)
        both = halves(change_ref[:, col])
        spots = spot_ref[q : q + 1, :]
        low = jnp.broadcast_to((spots & (PAIR - 1)).astype(BF16), (PAIR, 128))
        b_ref[:, col] = jnp.where(low == within_of, jnp.bfloat16(1), zero)
        which = jnp.broadcast_to((spots >> 8).astype(BF16), (16, 128))
        for r in range(blocks):
            a_ref[r * 16 : (r + 1) * 16, col] = jnp.where(which == jnp.bfloat16(r), both, zero)
    spread = lax.dot_general(a_ref[...], b_ref[...], (((1,), (1,)), ((), ())), preferred_element_type=F32)
    for r in range(blocks):
        delta_ref[:, r * PAIR : (r + 1) * PAIR] = spread[r * 16 : r * 16 + 8] + spread[r * 16 + 8 : r * 16 + 16]
    sweep(delta_ref, edge)
    for s in range(count):
        col = slice(s * NODES, (s + 1) * NODES)
        spot = pl.ds(pl.multiple_of(meta_ref[s] * NODES, NODES), NODES)
        out_ref[:, spot] = grid_ref[:, col] + delta_ref[:, col]

    @pl.when(meta_ref[31] > 0)
    def _():
        pltpu.sync_copy(value_hbm, delta_ref)
        general_table(map_hbm, delta_ref, map_smem, rows_ref, table_ref)
        pltpu.sync_copy(node_hbm, node_smem)
        to_rows(change_ref, rows_ref)
        spare = table_ref.shape[0] - 1

        def bury(i, carry):
            p = i // slot_count
            node_smem[i] = jnp.where(i - p * slot_count < count_ref[p], node_smem[i], spare)
            return carry

        lax.fori_loop(0, slots_all, bury, 0)
        add_rows(node_smem, rows_ref, table_ref)
        take_rows(map_smem, table_ref, rows_ref)

        def put(base, block):
            out_ref[:, pl.ds(base, 128)] = block

        from_rows(rows_ref, out_ref, put)


def exchange_kernel(
    groups, places, picked_ref, owned_ref, change_ref,
    inbox, reply, back, a_ref, b_ref, send_out, recv_out, send_back, recv_back,
):
    fields, slots_all = picked_ref.shape
    size = slots_all // (3 * places)
    heads = a_ref.shape[0] // 16
    g, l = lax.axis_index("grp"), lax.axis_index("loc")
    reach = [(g + k - 1 >= 0) & (g + k - 1 < groups) for k in range(3)]
    heard = [(g - k + 1 >= 0) & (g - k + 1 < groups) for k in range(3)]
    peers = [(k, d) for d in range(places) for k in range(3) if (k, d) != (1, 0)]

    def part(k, place):
        return pl.ds(pl.multiple_of((k * places + place) * size, 128), size)

    def ahead(d):
        return lax.rem(l + d, places)

    def behind(d):
        return lax.rem(l + places - d, places)

    def outward(k, d):
        return pltpu.make_async_remote_copy(
            src_ref=picked_ref.at[:, part(k, ahead(d))],
            dst_ref=inbox.at[:, part(k, l)],
            send_sem=send_out.at[k * places + d],
            recv_sem=recv_out.at[k * places + d],
            device_id=(g + k - 1, ahead(d)),
            device_id_type=MESH,
        )

    def homeward(k, d):
        return pltpu.make_async_remote_copy(
            src_ref=reply.at[:, part(k, behind(d))],
            dst_ref=back.at[:, part(k, l)],
            send_sem=send_back.at[k * places + d],
            recv_sem=recv_back.at[k * places + d],
            device_id=(g - k + 1, behind(d)),
            device_id_type=MESH,
        )

    def outward_in(k, d):
        return pltpu.make_async_remote_copy(
            src_ref=picked_ref.at[:, part(k, ahead(d))],
            dst_ref=inbox.at[:, part(k, behind(d))],
            send_sem=send_out.at[k * places + d],
            recv_sem=recv_out.at[k * places + d],
            device_id=(g, l),
            device_id_type=MESH,
        )

    def homeward_in(k, d):
        return pltpu.make_async_remote_copy(
            src_ref=reply.at[:, part(k, behind(d))],
            dst_ref=back.at[:, part(k, ahead(d))],
            send_sem=send_back.at[k * places + d],
            recv_sem=recv_back.at[k * places + d],
            device_id=(g, l),
            device_id_type=MESH,
        )

    barrier = pltpu.get_barrier_semaphore()
    for k, d in peers:

        @pl.when(reach[k])
        def _():
            pl.semaphore_signal(barrier, inc=1, device_id=(g + k - 1, ahead(d)), device_id_type=MESH)

    known = sum(r.astype(I32) for r in reach)
    pl.semaphore_wait(barrier, known * places - 1)

    for k, d in reversed(peers):

        @pl.when(reach[k])
        def _():
            outward(k, d).start()

    own = part(1, l)
    inbox[:, own] = picked_ref[:, own]
    for k in (0, 2):
        whole = slice(k * places * size, (k + 1) * places * size)

        @pl.when(jnp.logical_not(heard[k]))
        def _():
            inbox[:, whole] = jnp.zeros((fields, places * size), F32)

        @pl.when(jnp.logical_not(reach[k]))
        def _():
            back[:, whole] = jnp.zeros((fields, places * size), F32)

    zero = jnp.bfloat16(0)
    within_of = iota((128, 128), 0).astype(BF16)
    for q in range(slots_all // 128):
        low = jnp.broadcast_to((owned_ref[q : q + 1, :] & 127).astype(BF16), (128, 128))
        b_ref[:, q * 128 : (q + 1) * 128] = jnp.where(low == within_of, jnp.bfloat16(1), zero)

    for k, d in peers:

        @pl.when(heard[k])
        def _():
            outward_in(k, d).wait_recv()

    for q in range(slots_all // 128):
        col = slice(q * 128, (q + 1) * 128)
        both = halves(inbox[:, col])
        which = jnp.broadcast_to((owned_ref[q : q + 1, :] >> 7).astype(BF16), (16, 128))
        for h in range(heads):
            a_ref[h * 16 : (h + 1) * 16, col] = jnp.where(which == jnp.bfloat16(h), both, zero)
    summed = lax.dot_general(a_ref[...], b_ref[...], (((1,), (1,)), ((), ())), preferred_element_type=F32)
    totals = [summed[h * 16 : h * 16 + 8] + summed[h * 16 + 8 : h * 16 + 16] for h in range(heads)]
    for q in range(slots_all // 128):
        col = slice(q * 128, (q + 1) * 128)
        owned = jnp.broadcast_to(owned_ref[q : q + 1, :], (fields, 128))
        low, which = owned & 127, owned >> 7
        total = jnp.zeros((fields, 128), F32)
        for h in range(heads):
            total = jnp.where(which == h, jnp.take_along_axis(totals[h], low, axis=1), total)
        reply[:, col] = total

    for k, d in reversed(peers):

        @pl.when(heard[k])
        def _():
            homeward(k, d).start()

    back[:, own] = reply[:, own]
    for k, d in peers:

        @pl.when(reach[k])
        def _():
            homeward_in(k, d).wait_recv()

    change_ref[...] = back[...] - picked_ref[...]
    for k, d in peers:

        @pl.when(reach[k])
        def _():
            outward(k, d).wait_send()

        @pl.when(heard[k])
        def _():
            homeward(k, d).wait_send()


SMEM = pl.BlockSpec(memory_space=pltpu.SMEM)
VMEM = pl.BlockSpec(memory_space=pltpu.VMEM)
ANY = pl.BlockSpec(memory_space=pl.ANY)


def on_device(groups, places, element_values, local_map, send_node, send_count, recv_slot):
    fields, span = element_values.shape
    slots_all = send_node.shape[1]
    slot_count = slots_all // (3 * places)
    owned = 2 * slot_count
    edge = blocks_along(span)
    local = ((SIDE - 1) * edge + 1) ** 3
    tall16 = (local + 2047) // 2048 * 16
    table = (local + 96) // 96 * 96
    lines, slot_rows = span // 128, slots_all // 128
    params = pltpu.CompilerParams(vmem_limit_bytes=48 * 1024 * 1024)
    nodes, counts = send_node[0], send_count[0]
    general = [
        pltpu.SMEM((span,), I32),
        pltpu.SMEM((slots_all,), I32),
        pltpu.VMEM((span, 128), F32),
        pltpu.VMEM((table, 128), F32),
    ]
    picked, grid, spots, meta = pl.pallas_call(
        functools.partial(assemble_kernel, edge, slot_count),
        out_shape=(
            jax.ShapeDtypeStruct((fields, slots_all), F32),
            jax.ShapeDtypeStruct((fields, span), F32),
            jax.ShapeDtypeStruct((slot_rows, 128), I32),
            jax.ShapeDtypeStruct((32,), I32),
        ),
        in_specs=[VMEM, VMEM, VMEM, SMEM, ANY, ANY],
        out_specs=(VMEM, VMEM, VMEM, SMEM),
        scratch_shapes=[
            pltpu.VMEM((32 * ROWS, 128), I32),
            pltpu.VMEM((lines, 128), I32),
            pltpu.VMEM((2 * tall16, span), BF16),
            pltpu.VMEM((128, span), BF16),
            pltpu.VMEM((lines // 2 * 16, PAIR), BF16),
        ]
        + general,
        compiler_params=params,
    )(element_values, local_map.reshape(lines, 128), nodes.reshape(slot_rows, 128), counts, local_map, nodes)
    change = pl.pallas_call(
        functools.partial(exchange_kernel, groups, places),
        out_shape=jax.ShapeDtypeStruct((fields, slots_all), F32),
        in_specs=[VMEM, VMEM],
        out_specs=VMEM,
        scratch_shapes=[pltpu.VMEM((fields, slots_all), F32)] * 3
        + [
            pltpu.VMEM((owned // 128 * 16, slots_all), BF16),
            pltpu.VMEM((128, slots_all), BF16),
        ]
        + [pltpu.SemaphoreType.DMA((3 * places,))] * 4,
        compiler_params=pltpu.CompilerParams(collective_id=0, has_side_effects=True),
    )(picked, recv_slot[0].reshape(slot_rows, 128))
    return pl.pallas_call(
        functools.partial(finish_kernel, edge, slot_count),
        out_shape=jax.ShapeDtypeStruct((fields, span), F32),
        in_specs=[VMEM, VMEM, VMEM, SMEM, SMEM, ANY, ANY, ANY],
        out_specs=VMEM,
        scratch_shapes=[
            pltpu.VMEM((fields, span), F32),
            pltpu.VMEM((lines // 2 * 16, slots_all), BF16),
            pltpu.VMEM((PAIR, slots_all), BF16),
        ]
        + general,
        compiler_params=params,
    )(change, spots, grid, meta, counts, element_values, local_map, nodes)


def solution(mesh):
    return jax.shard_map(
        functools.partial(on_device, mesh.shape["grp"], mesh.shape["loc"]),
        mesh=mesh,
        in_specs=(
            P(None, ("grp", "loc")),
            P(("grp", "loc")),
            P(("grp", "loc"), None),
            P(("grp", "loc"), None),
            P(("grp", "loc"), None),
        ),
        out_specs=P(None, ("grp", "loc")),
        check_vma=False,
    )
```

time: 141 us -> 33.1 us (0.23)
  Pallas kernels: 61.8 us -> 27.8 us
  other arithmetic: 20.6 us -> 0 us
  starting transfers between devices: 17.4 us -> 0 us
  local copies, waits for them, and re-layouts: 21.4 us -> 4.72 us
  waiting for transfers between devices: 11.1 us -> 0 us
  blocking collectives: 7.32 us -> 0 us
    pallas_call x2 -> x3, Pallas kernels: 61.8 us -> 27.8 us  [the longest x1 16.1 us: on_device(): pl.pallas_call(functools.partial(exchange_kernel, groups, places), out_sh...]
    scatter-add x1 -> x0, other arithmetic: 17 us -> none  [on_device(): jnp.zeros((fields, owned_count), jnp.float32).at[:, targets]]
    ppermute x4 -> x0, starting transfers between devices: 12.8 us -> none  [shifted(): return lax.ppermute(block, axis, route)]
    gather x1 -> x0, local copies, waits for them, and re-layouts: 8.11 us -> none  [on_device(): totals.at[:, targets].get(mode='promise_in_bounds')]
    all_to_all x1 -> x0, blocking collectives: 7.32 us -> none  [within_outward(): lax.all_to_all(buffer, 'loc', split_axis=2, concat_axis=2, tiled=True)]
    ppermute x4 -> x0, waiting for transfers between devices: 6.4 us -> none  [shifted(): return lax.ppermute(block, axis, route)]
    transpose x1 -> x0, local copies, waits for them, and re-layouts: 5.4 us -> none  [on_device(): return summed.T]
    all_to_all x1 -> x0, waiting for transfers between devices: 4.68 us -> none  [within_inward(): lax.all_to_all(buffer, 'loc', split_axis=2, concat_axis=2, tiled=True)]
  transfers between devices with their start and end apart: 5 -> 0, of which waited for: 3 -> 0; matrix products, arithmetic and copies ran while one was open for 0% -> 0% of each run, Pallas kernels for 0% -> 0%
where the time goes in v1:
time: 33.1 us; the launch traced here: 32.6 us
  Pallas kernels  27.8 us (84%)
  local copies, waits for them, and re-layouts  4.72 us (14%)
    pallas_call x1, Pallas kernels, on_device(): pl.pallas_call(functools.partial(exchange_kernel, groups, places), out_sh...  16.1 us
    pallas_call x1, Pallas kernels, on_device(): pl.pallas_call(functools.partial(assemble_kernel, edge, slot_count), out_...  8.38 us
    unnamed x18, local copies, waits for them, and re-layouts  4.72 us
    pallas_call x1, Pallas kernels, on_device(): pl.pallas_call(functools.partial(finish_kernel, edge, slot_count), out_sh...  3.33 us

profile of v1, /device:TPU:1, one launch (start us, length us, event | category | flops | bytes accessed | tf_op | source)
XLA Modules:
  0.0 32.6 jit_solution(6277737392444664599)
XLA Ops:
  0.0 0.0 copy-start.8
  0.0 0.7 %copy-done.8 = s32[1,12]{1,0:T(1,128)S(1)} copy-done((s32[1,12]{1,0:T(1,128)S(1)}, s32[1,12]{1,0:T(1,128)}, u32[]{:S(2)}) %copy-start.8) | copy-done | bytes 72
  0.7 0.0 copy-start
  0.7 1.0 %copy-done = f32[8,13824]{1,0:T(8,128)S(1)} copy-done((f32[8,13824]{1,0:T(8,128)S(1)}, f32[8,13824]{1,0:T(8,128)}, u32[]{:S(2)}) %copy-start) | copy-done | bytes 442392
  1.7 0.0 copy-start.2
  1.7 0.8 %copy-done.2 = s32[13824]{0:T(1024)S(1)} copy-done((s32[13824]{0:T(1024)S(1)}, s32[13824]{0:T(1024)}, u32[]{:S(2)}) %copy-start.2) | copy-done | bytes 55320
  2.5 0.0 copy-start.5
  2.5 0.7 %copy-done.5 = s32[1,3072]{1,0:T(1,128)S(1)} copy-done((s32[1,3072]{1,0:T(1,128)S(1)}, s32[1,3072]{1,0:T(1,128)}, u32[]{:S(2)}) %copy-start.5) | copy-done | bytes 12312
  3.2 0.0 copy-start.1
  3.2 8.4 %shard_map.55 = (f32[8,3072]{1,0:T(8,128)S(1)}, f32[8,13824]{1,0:T(8,128)S(1)}, s32[24,128]{1,0:T(8,128)S(1)}, s32[32]{0:T(128)S(1)}) custom-call(f32[8,13824]{1,0:T(8,128)S(1)} %copy-done, s32[108,128]{1,0:T(8,128)S(1)} %bitcast.5, s32[24,128]{1,0:T(8,128)S(1)} %bitcast.6, s32[12]{0:T(128)S(1)} %bitcast.9, s32[13824]{0:T(1024)S(1)} %copy-done.2, ...), custom_call_target="tpu_custom_call" | custom-call | tf_op jit(solution)/shard_map/pallas_call | solution.py:504
  11.6 0.0 copy-start.7
  11.6 0.6 %copy-done.7 = f32[8,3072]{1,0:T(8,128)} copy-done((f32[8,3072]{1,0:T(8,128)}, f32[8,3072]{1,0:T(8,128)S(1)}, u32[]{:S(2)}) %copy-start.7) | copy-done | bytes 98328
  12.2 0.0 copy-start.3
  12.2 0.0 copy-start.6
  12.2 16.1 %shard_map.56.change_ref = f32[8,3072]{1,0:T(8,128)} custom-call(f32[8,3072]{1,0:T(8,128)} %copy-done.7, s32[24,128]{1,0:T(8,128)} %bitcast.11), custom_call_target="tpu_custom_call" | custom-call | tf_op jit(solution)/shard_map/pallas_call | solution.py:524
  28.3 0.0 copy-done.1
  28.3 0.0 copy-done.3
  28.3 0.0 copy-done.6
  28.4 0.0 copy-start.4
  28.4 0.9 %copy-done.4 = f32[8,3072]{1,0:T(8,128)S(1)} copy-done((f32[8,3072]{1,0:T(8,128)S(1)}, f32[8,3072]{1,0:T(8,128)}, u32[]{:S(2)}) %copy-start.4) | copy-done | bytes 98328
  29.2 3.3 %shard_map.57 = f32[8,13824]{1,0:T(8,128)} custom-call(f32[8,3072]{1,0:T(8,128)S(1)} %copy-done.4, s32[24,128]{1,0:T(8,128)S(1)} %get-tuple-element.10.spot_ref, f32[8,13824]{1,0:T(8,128)S(1)} %get-tuple-element.11.grid_ref, s32[32]{0:T(128)S(1)} %get-tuple-element.12.meta_ref, s32[12]{0:T(128)S(1)} %bitcast.10, f32[8,13824]{1,0:T(8,128)S(1)} %copy-done.1, ...), custom_call_target="tpu_custom_call" | custom-call | tf_op jit(solution)/shard_map/pallas_call | solution.py:537
Async XLA Ops:
  0.0 0.7 %copy-start.8 = (s32[1,12]{1,0:T(1,128)S(1)}, s32[1,12]{1,0:T(1,128)}, u32[]{:S(2)}) copy-start(s32[1,12]{1,0:T(1,128)} %param.8) | copy-start | bytes 148
  0.7 1.0 %copy-start = (f32[8,13824]{1,0:T(8,128)S(1)}, f32[8,13824]{1,0:T(8,128)}, u32[]{:S(2)}) copy-start(f32[8,13824]{1,0:T(8,128)} %value_hbm.1) | copy-start | bytes 1327108
  1.7 0.8 %copy-start.2 = (s32[13824]{0:T(1024)S(1)}, s32[13824]{0:T(1024)}, u32[]{:S(2)}) copy-start(s32[13824]{0:T(1024)} %map_hbm.3) | copy-start | bytes 165892
  2.5 0.7 %copy-start.5 = (s32[1,3072]{1,0:T(1,128)S(1)}, s32[1,3072]{1,0:T(1,128)}, u32[]{:S(2)}) copy-start(s32[1,3072]{1,0:T(1,128)} %param.7) | copy-start | bytes 36868
  3.2 25.1 %copy-start.1 = (f32[8,13824]{1,0:T(8,128)S(1)}, f32[8,13824]{1,0:T(8,128)}, u32[]{:S(2)}) copy-start(f32[8,13824]{1,0:T(8,128)} %value_hbm.1) | copy-start | bytes 1327108
  11.6 0.6 %copy-start.7 = (f32[8,3072]{1,0:T(8,128)}, f32[8,3072]{1,0:T(8,128)S(1)}, u32[]{:S(2)}) copy-start(f32[8,3072]{1,0:T(8,128)S(1)} %get-tuple-element.9.picked_ref) | copy-start | bytes 294916
  12.2 16.1 %copy-start.3 = (s32[13824]{0:T(1024)S(1)}, s32[13824]{0:T(1024)}, u32[]{:S(2)}) copy-start(s32[13824]{0:T(1024)} %map_hbm.3) | copy-start | bytes 165892
  12.2 16.1 %copy-start.6 = (s32[1,3072]{1,0:T(1,128)S(1)}, s32[1,3072]{1,0:T(1,128)}, u32[]{:S(2)}) copy-start(s32[1,3072]{1,0:T(1,128)} %param.7) | copy-start | bytes 36868
  28.4 0.9 %copy-start.4 = (f32[8,3072]{1,0:T(8,128)S(1)}, f32[8,3072]{1,0:T(8,128)}, u32[]{:S(2)}) copy-start(f32[8,3072]{1,0:T(8,128)} %shard_map.56.change_ref) | copy-start | bytes 294916

commit v2 on v1

v2 whole, which is shorter than its diff:
```python
import functools

import jax
import jax.numpy as jnp
from jax import lax
from jax.experimental import pallas as pl
from jax.experimental.pallas import tpu as pltpu
from jax.sharding import PartitionSpec as P

MESH = pl.DeviceIdType.MESH
F32, BF16, I32 = jnp.float32, jnp.bfloat16, jnp.int32
SIDE = 8
NODES = SIDE**3
ROWS = NODES // 128
PAIR = 256
BATCH = 32


def blocks_along(span):
    edge = round((span // NODES) ** (1 / 3))
    assert edge**3 * NODES == span and 1 < edge <= 3
    return edge


def iota(shape, axis):
    return lax.broadcasted_iota(I32, shape, axis)


def halves(x):
    high = x.astype(BF16)
    low = (x - high.astype(F32)).astype(BF16)
    return jnp.concatenate([high, low], axis=0)


def add_rows(index_ref, value_ref, table_ref):
    def step(b, carry):
        base = pl.multiple_of(b * BATCH, BATCH)
        nodes = [index_ref[base + k] for k in range(BATCH)]
        held = [table_ref[pl.ds(n, 1), :] for n in nodes]
        sums = [held[k] + value_ref[pl.ds(base + k, 1), :] for k in range(BATCH)]
        for k in range(BATCH):
            table_ref[pl.ds(nodes[k], 1), :] = sums[k]
        return carry

    lax.fori_loop(0, index_ref.shape[0] // BATCH, step, 0)


def take_rows(index_ref, table_ref, out_ref):
    def step(b, carry):
        base = pl.multiple_of(b * BATCH, BATCH)
        rows = [table_ref[pl.ds(index_ref[base + k], 1), :] for k in range(BATCH)]
        for k in range(BATCH):
            out_ref[pl.ds(base + k, 1), :] = rows[k]
        return carry

    lax.fori_loop(0, index_ref.shape[0] // BATCH, step, 0)


def to_rows(flat_ref, rows_ref):
    def step(t, carry):
        base = pl.multiple_of(t * 128, 128)
        block = flat_ref[:, pl.ds(base, 128)]
        wide = jnp.concatenate([block] * (128 // block.shape[0]), axis=0)
        rows_ref[pl.ds(base, 128), :] = wide.T
        return carry

    lax.fori_loop(0, flat_ref.shape[1] // 128, step, 0)


def from_rows(rows_ref, flat_ref, put):
    def step(t, carry):
        base = pl.multiple_of(t * 128, 128)
        put(base, rows_ref[pl.ds(base, 128), :].T[: flat_ref.shape[0]])
        return carry

    lax.fori_loop(0, flat_ref.shape[1] // 128, step, 0)


def general_table(map_hbm, value_ref, map_smem, rows_ref, table_ref):
    pltpu.sync_copy(map_hbm, map_smem)
    chunk = 96

    def clear(b, carry):
        base = pl.multiple_of(b * chunk, chunk)
        table_ref[pl.ds(base, chunk), :] = jnp.zeros((chunk, 128), F32)
        return carry

    lax.fori_loop(0, table_ref.shape[0] // chunk, clear, 0)
    to_rows(value_ref, rows_ref)
    add_rows(map_smem, rows_ref, table_ref)


def sweep(ref, edge, base=None, out=None):
    lane = iota((ref.shape[0], 128), 1)
    zero = jnp.zeros((ref.shape[0], 128), F32)

    def at(px, py, pz, row):
        return pl.ds((((px * edge + py) * edge + pz) * ROWS + row) * 128, 128)

    def line(spots_of, first, last, shift, final=False):
        held = [ref[:, s] for s in spots_of]
        for i, s in enumerate(spots_of):
            total = held[i]
            if i + 1 < edge:
                total = total + jnp.where(last, pltpu.roll(held[i + 1], shift, 1), zero)
            if i > 0:
                total = total + jnp.where(first, pltpu.roll(held[i - 1], 128 - shift, 1), zero)
            if final and base is not None:
                out[:, s] = total + base[:, s]
            else:
                ref[:, s] = total

    for py in range(edge):
        for pz in range(edge):
            for px in range(edge - 1):
                a, b = at(px, py, pz, ROWS - 1), at(px + 1, py, pz, 0)
                upper, lower = ref[:, a], ref[:, b]
                ref[:, a] = upper + jnp.where(lane >= 64, pltpu.roll(lower, 64, 1), zero)
                ref[:, b] = lower + jnp.where(lane < 64, pltpu.roll(upper, 64, 1), zero)
    y, z = (lane // SIDE) % SIDE, lane % SIDE
    for px in range(edge):
        for pz in range(edge):
            for row in range(ROWS):
                line([at(px, py, pz, row) for py in range(edge)], y == 0, y == SIDE - 1, SIDE * (SIDE - 1))
    for px in range(edge):
        for py in range(edge):
            for row in range(ROWS):
                line([at(px, py, pz, row) for pz in range(edge)], z == 0, z == SIDE - 1, SIDE - 1, True)


def find_places(lab_ref, edge):
    count = edge**3
    near, mid, far = (lab_ref[pl.ds(k, 32, stride=ROWS), :].astype(F32) for k in (0, 1, ROWS - 1))
    near_t, mid_t, far_t = near.T, mid.T, far.T
    real = (iota((32, 32), 0) < count) & (iota((32, 32), 1) < count)
    sides = (
        (near, near_t, 27, far, far_t, 91),
        (mid, mid_t, 67, mid, mid_t, 123),
        (mid, mid_t, 88, mid, mid_t, 95),
    )
    place = jnp.zeros((32, 1), F32)
    for low, low_t, i, high, high_t, j in sides:
        before = jnp.where(real & (low[:, i : i + 1] == high_t[j : j + 1, :]), 1.0, 0.0)
        before_t = jnp.where(real & (high[:, j : j + 1] == low_t[i : i + 1, :]), 1.0, 0.0)
        steps = jnp.zeros((1, 32), F32)
        if edge > 2:
            steps = jnp.sum(before_t, axis=0, keepdims=True)
        place = place * edge + jnp.sum(before * (1.0 + steps), axis=1, keepdims=True)
    hit = (iota((32, 32), 0) < count) & (place == iota((32, 32), 1).astype(F32))
    who = jnp.sum(jnp.where(hit, iota((32, 32), 0).astype(F32), 0.0), axis=0, keepdims=True)
    times = jnp.sum(jnp.where(hit, 1.0, 0.0), axis=0, keepdims=True)
    wrong = jnp.where((iota((1, 32), 1) < count) & (times != 1.0), 1, 0)
    return jnp.clip(who.astype(I32), 0, count - 1), wrong


def count_mismatches(grid_ref, edge):
    total = jnp.zeros((1, 128), I32)
    lane = iota((1, 128), 1)
    y, z = (lane // SIDE) % SIDE, lane % SIDE
    for axis, stride in enumerate((edge * edge, edge, 1)):
        rows = (edge**3 - stride) * ROWS
        start = stride * ROWS - (ROWS - 1 if axis == 0 else 0)
        inner = (iota((rows, 1), 0) // ROWS // stride) % edge < edge - 1
        if axis == 0:
            where, shift = inner & (iota((rows, 1), 0) % ROWS == ROWS - 1) & (lane < 64), 64
        elif axis == 1:
            where, shift = inner & (y == 0), 128 - SIDE * (SIDE - 1)
        else:
            where, shift = inner & (z == 0), 128 - (SIDE - 1)
        low, high = grid_ref[0:rows, :], grid_ref[start : start + rows, :]
        differ = where & (pltpu.roll(low, shift, 1) != high)
        total = total + jnp.sum(jnp.where(differ, 1, 0), axis=0, keepdims=True)
    return total


def assemble_kernel(
    edge, slot_count, value_hbm, map_hbm, node_hbm, count_hbm, map_flat, node_flat,
    grid_ref, order_ref, node_ref, flag_ref, picked_ref,
    value_ref, lab_ref, raw_ref, count_ref, sems, map_smem, node_smem, rows_ref, table_ref,
):
    count = edge**3
    lines = order_ref.shape[0]
    slot_rows = node_ref.shape[0]
    labels = pltpu.make_async_copy(map_hbm, lab_ref.at[0:lines, :], sems.at[0])
    values = pltpu.make_async_copy(value_hbm, value_ref, sems.at[1])
    nodes = pltpu.make_async_copy(node_hbm, raw_ref, sems.at[2])
    counts = pltpu.make_async_copy(count_hbm, count_ref, sems.at[3])
    for copy in (labels, values, nodes, counts):
        copy.start()
    lab_ref[lines:, :] = jnp.zeros((lab_ref.shape[0] - lines, 128), I32)
    labels.wait()
    who, wrong = find_places(lab_ref, edge)
    flag_ref[...] = jnp.zeros((8, 128), I32)
    flag_ref[0:1, 0:32] = who
    values.wait()
    for s in range(count):
        e = who[0, s]
        grid_ref[:, s * NODES : (s + 1) * NODES] = value_ref[:, pl.ds(pl.multiple_of(e * NODES, NODES), NODES)]
        for r in range(ROWS):
            order_ref[s * ROWS + r : s * ROWS + r + 1, :] = lab_ref[pl.ds(e * ROWS + r, 1), :]
    sweep(grid_ref, edge)
    bad = jnp.sum(count_mismatches(order_ref, edge)) + jnp.sum(wrong)
    nodes.wait()
    counts.wait()
    per = slot_count // 128
    row_of = iota((slot_rows, 128), 0)
    limit = jnp.zeros((slot_rows, 128), I32)
    for p in range(slot_rows // per):
        limit = jnp.where(row_of // per == p, count_ref[p], limit)
    live = (row_of % per) * 128 + iota((slot_rows, 128), 1) < limit
    node_ref[...] = jnp.where(live, raw_ref[...], -1)
    flag_ref[1:2, :] = jnp.full((1, 128), bad, I32)

    @pl.when(bad > 0)
    def _():
        general_table(map_flat, value_ref, map_smem, rows_ref, table_ref)
        pltpu.sync_copy(node_flat, node_smem)
        take_rows(node_smem, table_ref, rows_ref)

        def put(base, block):
            p = base // slot_count
            keep = base - p * slot_count + iota((8, 128), 1) < count_ref[p]
            picked_ref[:, pl.ds(base, 128)] = jnp.where(keep, block, 0.0)

        from_rows(rows_ref, picked_ref, put)


def finish_kernel(
    edge, slot_count, delta_in, grid_ref, flag_ref, change_ref, count_hbm, value_hbm, map_flat, node_flat,
    out_hbm,
    delta_ref, flags, count_ref, sems, map_smem, node_smem, rows_ref, table_ref,
):
    count = edge**3
    slots_all = change_ref.shape[1]
    marks = pltpu.make_async_copy(flag_ref, flags, sems.at[0])
    marks.start()
    sweep(delta_in, edge, grid_ref, delta_ref)
    marks.wait()
    copies = []
    for s in range(count):
        spot = pl.ds(pl.multiple_of(flags[0, s] * NODES, NODES), NODES)
        copy = pltpu.make_async_copy(delta_ref.at[:, s * NODES : (s + 1) * NODES], out_hbm.at[:, spot], sems.at[1])
        copy.start()
        copies.append(copy)
    pltpu.make_async_copy(delta_ref, out_hbm, sems.at[1]).wait()

    @pl.when(flags[1, 0] > 0)
    def _():
        pltpu.sync_copy(value_hbm, delta_ref)
        pltpu.sync_copy(count_hbm, count_ref)
        general_table(map_flat, delta_ref, map_smem, rows_ref, table_ref)
        pltpu.sync_copy(node_flat, node_smem)
        to_rows(change_ref, rows_ref)
        spare = table_ref.shape[0] - 1

        def bury(i, carry):
            p = i // slot_count
            node_smem[i] = jnp.where(i - p * slot_count < count_ref[p], node_smem[i], spare)
            return carry

        lax.fori_loop(0, slots_all, bury, 0)
        add_rows(node_smem, rows_ref, table_ref)
        take_rows(map_smem, table_ref, rows_ref)

        def put(base, block):
            delta_ref[:, pl.ds(base, 128)] = block

        from_rows(rows_ref, delta_ref, put)
        pltpu.sync_copy(delta_ref, out_hbm)


def find_nodes(edge, order_ref, a_ref, b_ref):
    lines = order_ref.shape[0]
    tall16 = a_ref.shape[0] // 2
    lane = iota((1, 128), 1)
    first = (lane >= 64, (lane // SIDE) % SIDE > 0, lane % SIDE > 0)
    high_of = iota((tall16, 128), 0).astype(BF16)
    low_of = iota((128, 128), 0).astype(BF16)
    zero = jnp.bfloat16(0)
    for r in range(lines):
        s = r // ROWS
        place = (s // (edge * edge), (s // edge) % edge, s % edge)
        label = order_ref[r : r + 1, :]
        for axis in range(3):
            if place[axis] > 0 and (axis > 0 or r % ROWS == 0):
                label = jnp.where(first[axis], label, -1)
        high = jnp.broadcast_to((label >> 7).astype(BF16), (tall16, 128))
        low = jnp.broadcast_to((label & 127).astype(BF16), (128, 128))
        col = slice(r * 128, (r + 1) * 128)
        within = jnp.broadcast_to((lane + (r % 2) * 128).astype(BF16), (tall16, 128))
        hit = high == high_of
        a_ref[0:tall16, col] = jnp.where(hit, jnp.bfloat16(r // 2), zero)
        a_ref[tall16:, col] = jnp.where(hit, within, zero)
        b_ref[:, col] = jnp.where(low == low_of, jnp.bfloat16(1), zero)
    found = lax.dot_general(a_ref[...], b_ref[...], (((1,), (1,)), ((), ())), preferred_element_type=F32)
    return found[0:tall16] * PAIR + found[tall16:]


def exchange_kernel(
    groups, places, edge, order_ref, grid_ref, node_ref, owned_ref, flag_ref, other_ref,
    delta_ref, change_ref,
    picked, inbox, reply, back, spot_ref, pa_ref, pb_ref, u_ref, ta_ref, tb_ref, sa_ref, sb_ref,
    send_out, recv_out, send_back, recv_back,
):
    fields, slots_all = change_ref.shape
    size = slots_all // (3 * places)
    heads = ta_ref.shape[0] // 16
    slot_rows = node_ref.shape[0]
    blocks = grid_ref.shape[1] // PAIR
    g, l = lax.axis_index("grp"), lax.axis_index("loc")
    hops = [s * d for d in range(places - 1, 0, -1) for s in (1, -1)] + [0]
    peers = [(k, d) for d in hops for k in (0, 2, 1) if (k, d) != (1, 0)]
    reach = {(k, d): (g + k - 1 >= 0) & (g + k - 1 < groups) & (l + d >= 0) & (l + d < places) for k, d in peers}
    heard = {(k, d): (g - k + 1 >= 0) & (g - k + 1 < groups) & (l - d >= 0) & (l - d < places) for k, d in peers}

    def part(k, place):
        return pl.ds(pl.multiple_of((k * places + place) * size, 128), size)

    def copy(k, d, src, dst, near, far, sems, device):
        index = k * (2 * places - 1) + d + places - 1
        return pltpu.make_async_remote_copy(
            src_ref=src.at[:, part(k, near)],
            dst_ref=dst.at[:, part(k, far)],
            send_sem=sems[0].at[index],
            recv_sem=sems[1].at[index],
            device_id=device,
            device_id_type=MESH,
        )

    out_sems, back_sems = (send_out, recv_out), (send_back, recv_back)
    barrier = pltpu.get_barrier_semaphore()
    known = jnp.int32(0)
    for k, d in peers:
        known = known + reach[k, d].astype(I32)

        @pl.when(reach[k, d])
        def _():
            pl.semaphore_signal(barrier, inc=1, device_id=(g + k - 1, l + d), device_id_type=MESH)

    zero = jnp.bfloat16(0)
    where_is = find_nodes(edge, order_ref, pa_ref, pb_ref)
    for r in range(blocks):
        u_ref[r * 16 : (r + 1) * 16, :] = halves(grid_ref[:, r * PAIR : (r + 1) * PAIR])
    node = node_ref[...]
    high, low = node >> 7, node & 127
    spot = jnp.full((slot_rows, 128), -float(PAIR), F32)
    for h in range((((SIDE - 1) * edge + 1) ** 3 + 127) // 128):
        row = jnp.broadcast_to(where_is[h : h + 1, :], (slot_rows, 128))
        spot = jnp.where(high == h, jnp.take_along_axis(row, low, axis=1), spot)
    spot_ref[...] = spot.astype(I32)
    within_of = iota((PAIR, PAIR), 0).astype(BF16)
    block_of = iota((blocks, 1, PAIR), 0)
    general = jnp.concatenate([flag_ref[1:2, :]] * (PAIR // 128), axis=1) > 0
    for n in range(slots_all // PAIR):
        col = slice(n * PAIR, (n + 1) * PAIR)
        spots = jnp.concatenate([spot_ref[2 * n : 2 * n + 1, :], spot_ref[2 * n + 1 : 2 * n + 2, :]], axis=1)
        low = jnp.broadcast_to((spots & (PAIR - 1)).astype(BF16), (PAIR, PAIR))
        onehot = jnp.where(low == within_of, jnp.bfloat16(1), zero)
        both = jnp.dot(u_ref[...], onehot, preferred_element_type=F32)
        which = jnp.broadcast_to(spots >> 8, (fields, PAIR))
        top = jnp.zeros((fields, PAIR), F32)
        rest = jnp.zeros((fields, PAIR), F32)
        for r in range(blocks):
            mine = which == r
            top = jnp.where(mine, both[r * 16 : r * 16 + 8], top)
            rest = jnp.where(mine, both[r * 16 + 8 : r * 16 + 16], rest)
        picked[:, col] = jnp.where(general, other_ref[:, col], top + rest)

    pl.semaphore_wait(barrier, known)
    for k, d in peers:

        @pl.when(reach[k, d])
        def _():
            copy(k, d, picked, inbox, l + d, l, out_sems, (g + k - 1, l + d)).start()

    own = part(1, l)
    inbox[:, own] = picked[:, own]
    for k in (0, 2):
        whole = slice(k * places * size, (k + 1) * places * size)

        @pl.when(jnp.logical_not(heard[k, 0]))
        def _():
            inbox[:, whole] = jnp.zeros((fields, places * size), F32)

        @pl.when(jnp.logical_not(reach[k, 0]))
        def _():
            back[:, whole] = jnp.zeros((fields, places * size), F32)

    owned_low = iota((128, 128), 0).astype(BF16)
    spot_low = iota((PAIR, 128), 0).astype(BF16)
    for q in range(slots_all // 128):
        col = slice(q * 128, (q + 1) * 128)
        low = jnp.broadcast_to((owned_ref[q : q + 1, :] & 127).astype(BF16), (128, 128))
        tb_ref[:, col] = jnp.where(low == owned_low, jnp.bfloat16(1), zero)
        low = jnp.broadcast_to((spot_ref[q : q + 1, :] & (PAIR - 1)).astype(BF16), (PAIR, 128))
        sb_ref[:, col] = jnp.where(low == spot_low, jnp.bfloat16(1), zero)

    for k, d in reversed(peers):

        @pl.when(heard[k, d])
        def _():
            copy(k, d, picked, inbox, l, l - d, out_sems, (g, l)).wait_recv()

    for q in range(slots_all // 128):
        col = slice(q * 128, (q + 1) * 128)
        both = halves(inbox[:, col])
        which = jnp.broadcast_to((owned_ref[q : q + 1, :] >> 7).astype(BF16), (16, 128))
        for h in range(heads):
            ta_ref[h * 16 : (h + 1) * 16, col] = jnp.where(which == jnp.bfloat16(h), both, zero)
    summed = lax.dot_general(ta_ref[...], tb_ref[...], (((1,), (1,)), ((), ())), preferred_element_type=F32)
    totals = [summed[h * 16 : h * 16 + 8] + summed[h * 16 + 8 : h * 16 + 16] for h in range(heads)]
    for q in range(slots_all // 128):
        col = slice(q * 128, (q + 1) * 128)
        owned = jnp.broadcast_to(owned_ref[q : q + 1, :], (fields, 128))
        low, which = owned & 127, owned >> 7
        total = jnp.zeros((fields, 128), F32)
        for h in range(heads):
            total = jnp.where(which == h, jnp.take_along_axis(totals[h], low, axis=1), total)
        reply[:, col] = total

    for k, d in peers:

        @pl.when(heard[k, d])
        def _():
            copy(k, d, reply, back, l - d, l, back_sems, (g - k + 1, l - d)).start()

    back[:, own] = reply[:, own]
    for k, d in reversed(peers):

        @pl.when(reach[k, d])
        def _():
            copy(k, d, reply, back, l, l + d, back_sems, (g, l)).wait_recv()

    for q in range(slots_all // 128):
        col = slice(q * 128, (q + 1) * 128)
        change = back[:, col] - picked[:, col]
        change_ref[:, col] = change
        both = halves(change)
        which = jnp.broadcast_to((spot_ref[q : q + 1, :] >> 8).astype(BF16), (16, 128))
        for r in range(blocks):
            sa_ref[r * 16 : (r + 1) * 16, col] = jnp.where(which == jnp.bfloat16(r), both, zero)
    spread = lax.dot_general(sa_ref[...], sb_ref[...], (((1,), (1,)), ((), ())), preferred_element_type=F32)
    for r in range(blocks):
        delta_ref[:, r * PAIR : (r + 1) * PAIR] = spread[r * 16 : r * 16 + 8] + spread[r * 16 + 8 : r * 16 + 16]

    for k, d in peers:

        @pl.when(reach[k, d])
        def _():
            copy(k, d, picked, inbox, l + d, l, out_sems, (g, l)).wait_send()

        @pl.when(heard[k, d])
        def _():
            copy(k, d, reply, back, l - d, l, back_sems, (g, l)).wait_send()


SMEM = pl.BlockSpec(memory_space=pltpu.SMEM)
VMEM = pl.BlockSpec(memory_space=pltpu.VMEM)
HBM = pl.BlockSpec(memory_space=pltpu.HBM)


def on_device(groups, places, element_values, local_map, send_node, send_count, recv_slot):
    fields, span = element_values.shape
    slots_all = send_node.shape[1]
    slot_count = slots_all // (3 * places)
    owned = 2 * slot_count
    edge = blocks_along(span)
    local = ((SIDE - 1) * edge + 1) ** 3
    tall16 = (local + 2047) // 2048 * 16
    table = (local + 96) // 96 * 96
    lines, slot_rows = span // 128, slots_all // 128
    map_rows, node_rows = local_map.reshape(-1, 128), send_node.reshape(-1, 128)
    owned_rows = recv_slot.reshape(-1, 128)
    element_values, local_map, map_rows, node_rows, nodes, counts = (
        pltpu.with_memory_space_constraint(x, pltpu.HBM)
        for x in (element_values, local_map, map_rows, node_rows, send_node.reshape(-1), send_count.reshape(-1))
    )
    shape = jax.ShapeDtypeStruct
    general = [
        pltpu.SMEM((span,), I32),
        pltpu.SMEM((slots_all,), I32),
        pltpu.VMEM((span, 128), F32),
        pltpu.VMEM((table, 128), F32),
    ]
    grid, order, live_nodes, flags, other = pl.pallas_call(
        functools.partial(assemble_kernel, edge, slot_count),
        out_shape=(
            shape((fields, span), F32),
            shape((lines, 128), I32),
            shape((slot_rows, 128), I32),
            shape((8, 128), I32),
            shape((fields, slots_all), F32),
        ),
        in_specs=[HBM] * 6,
        out_specs=(VMEM,) * 5,
        scratch_shapes=[
            pltpu.VMEM((fields, span), F32),
            pltpu.VMEM((32 * ROWS, 128), I32),
            pltpu.VMEM((slot_rows, 128), I32),
            pltpu.SMEM(counts.shape, I32),
            pltpu.SemaphoreType.DMA((4,)),
        ]
        + general,
        compiler_params=pltpu.CompilerParams(vmem_limit_bytes=24 * 1024 * 1024),
    )(element_values, map_rows, node_rows, counts, local_map, nodes)
    delta, change = pl.pallas_call(
        functools.partial(exchange_kernel, groups, places, edge),
        out_shape=(shape((fields, span), F32), shape((fields, slots_all), F32)),
        in_specs=[VMEM] * 6,
        out_specs=(VMEM, VMEM),
        scratch_shapes=[pltpu.VMEM((fields, slots_all), F32)] * 4
        + [
            pltpu.VMEM((slot_rows, 128), I32),
            pltpu.VMEM((2 * tall16, span), BF16),
            pltpu.VMEM((128, span), BF16),
            pltpu.VMEM((lines // 2 * 16, PAIR), BF16),
            pltpu.VMEM((owned // 128 * 16, slots_all), BF16),
            pltpu.VMEM((128, slots_all), BF16),
            pltpu.VMEM((lines // 2 * 16, slots_all), BF16),
            pltpu.VMEM((PAIR, slots_all), BF16),
        ]
        + [pltpu.SemaphoreType.DMA((3 * (2 * places - 1),))] * 4,
        compiler_params=pltpu.CompilerParams(
            collective_id=0, has_side_effects=True, vmem_limit_bytes=40 * 1024 * 1024
        ),
    )(order, grid, live_nodes, owned_rows, flags, other)
    return pl.pallas_call(
        functools.partial(finish_kernel, edge, slot_count),
        out_shape=shape((fields, span), F32),
        in_specs=[VMEM] * 4 + [HBM] * 4,
        out_specs=HBM,
        scratch_shapes=[
            pltpu.VMEM((fields, span), F32),
            pltpu.SMEM((8, 128), I32),
            pltpu.SMEM(counts.shape, I32),
            pltpu.SemaphoreType.DMA((2,)),
        ]
        + general,
        compiler_params=pltpu.CompilerParams(vmem_limit_bytes=24 * 1024 * 1024),
    )(delta, grid, flags, change, counts, element_values, local_map, nodes)


def solution(mesh):
    return jax.shard_map(
        functools.partial(on_device, mesh.shape["grp"], mesh.shape["loc"]),
        mesh=mesh,
        in_specs=(
            P(None, ("grp", "loc")),
            P(("grp", "loc")),
            P(("grp", "loc"), None),
            P(("grp", "loc"), None),
            P(("grp", "loc"), None),
        ),
        out_specs=P(None, ("grp", "loc")),
        check_vma=False,
    )
```

time: 33.1 us -> 23.8 us (0.72); the launches traced: 32.6 us -> 23.7 us
  local copies, waits for them, and re-layouts: 4.72 us -> 0.01 us
  Pallas kernels: 27.8 us -> 23.7 us
    pallas_call x1, Pallas kernels: 8.38 us -> 1.8 us  [on_device(): pl.pallas_call(functools.partial(assemble_kernel, edge, slot_count), out_...]
    unnamed x18 -> x2, local copies, waits for them, and re-layouts: 4.72 us -> 0.01 us
    pallas_call x1, Pallas kernels: 16.1 us -> 20.5 us  [on_device(): pl.pallas_call(functools.partial(exchange_kernel, groups, places, edge),...]
    pallas_call x1, Pallas kernels: 3.33 us -> 1.37 us  [on_device(): pl.pallas_call(functools.partial(finish_kernel, edge, slot_count), out_sh...]
where the time goes in v2:
time: 23.8 us; the launch traced here: 23.7 us
  Pallas kernels  23.7 us (100%)
    pallas_call x1, Pallas kernels, on_device(): pl.pallas_call(functools.partial(exchange_kernel, groups, places, edge),...  20.5 us
    pallas_call x1, Pallas kernels, on_device(): pl.pallas_call(functools.partial(assemble_kernel, edge, slot_count), out_...  1.8 us
    pallas_call x1, Pallas kernels, on_device(): pl.pallas_call(functools.partial(finish_kernel, edge, slot_count), out_sh...  1.37 us

profile of v2, /device:TPU:1, one launch (start us, length us, event | category | flops | bytes accessed | tf_op | source)
XLA Modules:
  0.0 23.7 jit_solution(11832003922858960851)
XLA Ops:
  0.0 0.0 copy-start
  0.0 1.8 %shard_map.55 = (f32[8,13824]{1,0:T(8,128)S(1)}, s32[108,128]{1,0:T(8,128)S(1)}, s32[24,128]{1,0:T(8,128)S(1)}, s32[8,128]{1,0:T(8,128)S(1)}, f32[8,3072]{1,0:T(8,128)S(1)}) custom-call(f32[8,13824]{1,0:T(8,128)} %value_hbm.3, s32[108,128]{1,0:T(8,128)} %bitcast.6, s32[24,128]{1,0:T(8,128)} %bitcast.7, s32[12]{0:T(128)} %bitcast.10, s32[13824]{0:T(1024)} %map_flat.3, ...), custom_call_target="tpu_custom_call" | custom-call | tf_op jit(solution)/shard_map/pallas_call | solution.py:485
  1.8 0.0 copy-done
  1.8 20.5 %shard_map.56 = (f32[8,13824]{1,0:T(8,128)S(1)}, f32[8,3072]{1,0:T(8,128)S(1)}) custom-call(s32[108,128]{1,0:T(8,128)S(1)} %get-tuple-element.12.order_ref, f32[8,13824]{1,0:T(8,128)S(1)} %get-tuple-element.13.grid_ref, s32[24,128]{1,0:T(8,128)S(1)} %get-tuple-element.14.node_ref, s32[24,128]{1,0:T(8,128)S(1)} %bitcast.5, ...), custom_call_target="tpu_custom_call" | custom-call | tf_op jit(solution)/shard_map/pallas_call | solution.py:506
  22.3 1.4 %shard_map.57 = f32[8,13824]{1,0:T(8,128)} custom-call(f32[8,13824]{1,0:T(8,128)S(1)} %get-tuple-element.17.delta_in, f32[8,13824]{1,0:T(8,128)S(1)} %get-tuple-element.13.grid_ref, s32[8,128]{1,0:T(8,128)S(1)} %get-tuple-element.15.flag_ref, f32[8,3072]{1,0:T(8,128)S(1)} %get-tuple-element.18.change_ref, s32[12]{0:T(128)} %bitcast.11, ...), custom_call_target="tpu_custom_call" | custom-call | tf_op jit(solution)/shard_map/pallas_call | solution.py:527
Async XLA Ops:
  0.0 1.8 %copy-start = (s32[1,3072]{1,0:T(1,128)S(1)}, s32[1,3072]{1,0:T(1,128)}, u32[]{:S(2)}) copy-start(s32[1,3072]{1,0:T(1,128)} %param.9) | copy-start | bytes 36868

commit v3 on v2

--- a/solution.py
+++ b/solution.py
@@ -122,7 +122,6 @@
         for pz in range(edge):
             for row in range(ROWS):
                 line([at(px, py, pz, row) for py in range(edge)], y == 0, y == SIDE - 1, SIDE * (SIDE - 1))
-    for px in range(edge):
         for py in range(edge):
             for row in range(ROWS):
                 line([at(px, py, pz, row) for pz in range(edge)], z == 0, z == SIDE - 1, SIDE - 1, True)
@@ -173,19 +172,19 @@
     return total
 
 
-def assemble_kernel(
-    edge, slot_count, value_hbm, map_hbm, node_hbm, count_hbm, map_flat, node_flat,
-    grid_ref, order_ref, node_ref, flag_ref, picked_ref,
-    value_ref, lab_ref, raw_ref, count_ref, sems, map_smem, node_smem, rows_ref, table_ref,
+def order_kernel(
+    edge, slot_count, map_hbm, node_hbm, count_hbm, value_hbm, map_flat, node_flat,
+    order_ref, node_ref, flag_ref, picked_ref, grid_ref,
+    lab_ref, raw_ref, count_ref, sems, value_ref, map_smem, node_smem, rows_ref, table_ref,
 ):
     count = edge**3
     lines = order_ref.shape[0]
     slot_rows = node_ref.shape[0]
     labels = pltpu.make_async_copy(map_hbm, lab_ref.at[0:lines, :], sems.at[0])
-    values = pltpu.make_async_copy(value_hbm, value_ref, sems.at[1])
-    nodes = pltpu.make_async_copy(node_hbm, raw_ref, sems.at[2])
-    counts = pltpu.make_async_copy(count_hbm, count_ref, sems.at[3])
-    for copy in (labels, values, nodes, counts):
+    nodes = pltpu.make_async_copy(node_hbm, raw_ref, sems.at[1])
+    counts = pltpu.make_async_copy(count_hbm, count_ref, sems.at[2])
+    values = pltpu.make_async_copy(value_hbm, value_ref, sems.at[3])
+    for copy in (labels, nodes, counts, values):
         copy.start()
     lab_ref[lines:, :] = jnp.zeros((lab_ref.shape[0] - lines, 128), I32)
     labels.wait()
@@ -198,7 +197,6 @@
         grid_ref[:, s * NODES : (s + 1) * NODES] = value_ref[:, pl.ds(pl.multiple_of(e * NODES, NODES), NODES)]
         for r in range(ROWS):
             order_ref[s * ROWS + r : s * ROWS + r + 1, :] = lab_ref[pl.ds(e * ROWS + r, 1), :]
-    sweep(grid_ref, edge)
     bad = jnp.sum(count_mismatches(order_ref, edge)) + jnp.sum(wrong)
     nodes.wait()
     counts.wait()
@@ -236,12 +234,9 @@
     marks.start()
     sweep(delta_in, edge, grid_ref, delta_ref)
     marks.wait()
-    copies = []
     for s in range(count):
         spot = pl.ds(pl.multiple_of(flags[0, s] * NODES, NODES), NODES)
-        copy = pltpu.make_async_copy(delta_ref.at[:, s * NODES : (s + 1) * NODES], out_hbm.at[:, spot], sems.at[1])
-        copy.start()
-        copies.append(copy)
+        pltpu.make_async_copy(delta_ref.at[:, s * NODES : (s + 1) * NODES], out_hbm.at[:, spot], sems.at[1]).start()
     pltpu.make_async_copy(delta_ref, out_hbm, sems.at[1]).wait()
 
     @pl.when(flags[1, 0] > 0)
@@ -297,161 +292,186 @@
 
 
 def exchange_kernel(
-    groups, places, edge, order_ref, grid_ref, node_ref, owned_ref, flag_ref, other_ref,
-    delta_ref, change_ref,
+    groups, places, edge, order_ref, node_ref, owned_ref, flag_ref, other_ref, raw_ref,
+    grid_ref, delta_ref, change_ref,
     picked, inbox, reply, back, spot_ref, pa_ref, pb_ref, u_ref, ta_ref, tb_ref, sa_ref, sb_ref,
     send_out, recv_out, send_back, recv_back,
 ):
     fields, slots_all = change_ref.shape
     size = slots_all // (3 * places)
     heads = ta_ref.shape[0] // 16
-    slot_rows = node_ref.shape[0]
     blocks = grid_ref.shape[1] // PAIR
     g, l = lax.axis_index("grp"), lax.axis_index("loc")
-    hops = [s * d for d in range(places - 1, 0, -1) for s in (1, -1)] + [0]
-    peers = [(k, d) for d in hops for k in (0, 2, 1) if (k, d) != (1, 0)]
-    reach = {(k, d): (g + k - 1 >= 0) & (g + k - 1 < groups) & (l + d >= 0) & (l + d < places) for k, d in peers}
-    heard = {(k, d): (g - k + 1 >= 0) & (g - k + 1 < groups) & (l - d >= 0) & (l - d < places) for k, d in peers}
+
+    far = [jnp.where(m > l, m - l, l - m) for m in range(places)]
+    rank = [
+        sum(((far[n] > far[m]) | ((far[n] == far[m]) & (n > m))).astype(I32) for n in range(places) if n != m)
+        for m in range(places)
+    ]
+    places_by = [sum(jnp.where(rank[m] == i, m, 0) for m in range(places)) for i in range(places - 1)] + [l]
+
+    def group(k):
+        return lax.rem(g + groups + k, groups)
+
+    def others(i):
+        return (0, 2) if i == places - 1 else (0, 2, 1)
 
     def part(k, place):
         return pl.ds(pl.multiple_of((k * places + place) * size, 128), size)
 
-    def copy(k, d, src, dst, near, far, sems, device):
-        index = k * (2 * places - 1) + d + places - 1
+    def lines_of(k, place):
+        return [pl.ds((k * places + place) * (size // 128) + j, 1) for j in range(size // 128)]
+
+    def copy(k, src, dst, there, near, sems, device):
         return pltpu.make_async_remote_copy(
-            src_ref=src.at[:, part(k, near)],
-            dst_ref=dst.at[:, part(k, far)],
-            send_sem=sems[0].at[index],
-            recv_sem=sems[1].at[index],
+            src_ref=src.at[:, part(k, there)],
+            dst_ref=dst.at[:, part(k, near)],
+            send_sem=sems[0].at[k * places + there],
+            recv_sem=sems[1].at[k * places + near],
             device_id=device,
             device_id_type=MESH,
         )
 
-    out_sems, back_sems = (send_out, recv_out), (send_back, recv_back)
+    def outward(k, m):
+        return copy(k, picked, inbox, m, l, (send_out, recv_out), (group(k - 1), m))
+
+    def inward(k, m):
+        return copy(k, picked, inbox, m, m, (send_out, recv_out), (group(1 - k), m))
+
+    def homeward(k, m):
+        return copy(k, reply, back, m, l, (send_back, recv_back), (group(1 - k), m))
+
+    def returned(k, m):
+        return copy(k, reply, back, m, m, (send_back, recv_back), (group(k - 1), m))
+
     barrier = pltpu.get_barrier_semaphore()
-    known = jnp.int32(0)
-    for k, d in peers:
-        known = known + reach[k, d].astype(I32)
-
-        @pl.when(reach[k, d])
-        def _():
-            pl.semaphore_signal(barrier, inc=1, device_id=(g + k - 1, l + d), device_id_type=MESH)
+    for i in range(places):
+        for k in others(i):
+            pl.semaphore_signal(barrier, inc=1, device_id=(group(k - 1), places_by[i]), device_id_type=MESH)
 
     zero = jnp.bfloat16(0)
     where_is = find_nodes(edge, order_ref, pa_ref, pb_ref)
+    grid_ref[...] = raw_ref[...]
+    sweep(grid_ref, edge)
     for r in range(blocks):
         u_ref[r * 16 : (r + 1) * 16, :] = halves(grid_ref[:, r * PAIR : (r + 1) * PAIR])
-    node = node_ref[...]
-    high, low = node >> 7, node & 127
-    spot = jnp.full((slot_rows, 128), -float(PAIR), F32)
-    for h in range((((SIDE - 1) * edge + 1) ** 3 + 127) // 128):
-        row = jnp.broadcast_to(where_is[h : h + 1, :], (slot_rows, 128))
-        spot = jnp.where(high == h, jnp.take_along_axis(row, low, axis=1), spot)
-    spot_ref[...] = spot.astype(I32)
-    within_of = iota((PAIR, PAIR), 0).astype(BF16)
-    block_of = iota((blocks, 1, PAIR), 0)
-    general = jnp.concatenate([flag_ref[1:2, :]] * (PAIR // 128), axis=1) > 0
-    for n in range(slots_all // PAIR):
-        col = slice(n * PAIR, (n + 1) * PAIR)
-        spots = jnp.concatenate([spot_ref[2 * n : 2 * n + 1, :], spot_ref[2 * n + 1 : 2 * n + 2, :]], axis=1)
-        low = jnp.broadcast_to((spots & (PAIR - 1)).astype(BF16), (PAIR, PAIR))
-        onehot = jnp.where(low == within_of, jnp.bfloat16(1), zero)
-        both = jnp.dot(u_ref[...], onehot, preferred_element_type=F32)
-        which = jnp.broadcast_to(spots >> 8, (fields, PAIR))
-        top = jnp.zeros((fields, PAIR), F32)
-        rest = jnp.zeros((fields, PAIR), F32)
+    delta_ref[...] = jnp.zeros(delta_ref.shape, F32)
+
+    def spots_of(k, i):
+        row = i * (spot_ref.shape[0] // places) + k * (size // 128)
+        return jnp.concatenate([spot_ref[row + j : row + j + 1, :] for j in range(size // 128)], axis=1)
+
+    def owned_of(k, m):
+        return jnp.concatenate([owned_ref[line, :] for line in lines_of(k, m)], axis=1)
+
+    def onehot(index, count):
+        low = jnp.broadcast_to((index & (count - 1)).astype(BF16), (count, size))
+        return jnp.where(low == iota((count, size), 0).astype(BF16), jnp.bfloat16(1), zero)
+
+    tall = (((SIDE - 1) * edge + 1) ** 3 + 127) // 128
+
+    def look_up(i, m):
+        rows = [line for k in range(3) for line in lines_of(k, m)]
+        spare = [jnp.full((8 - len(rows) % 8, 128), -1, I32)] if len(rows) % 8 else []
+        node = jnp.concatenate([node_ref[line, :] for line in rows] + spare, axis=0)
+        high, low = node >> 7, node & 127
+        spot = jnp.full(node.shape, -float(PAIR), F32)
+        for h in range(tall):
+            row = jnp.broadcast_to(where_is[h : h + 1, :], node.shape)
+            spot = jnp.where(high == h, jnp.take_along_axis(row, low, axis=1), spot)
+        spot_ref[i * spot.shape[0] : (i + 1) * spot.shape[0], :] = spot.astype(I32)
+
+    def pick_by_lane(spots):
+        parts = []
+        for j in range(size // 128):
+            index = jnp.broadcast_to(spots[:, j * 128 : (j + 1) * 128], (fields, 128))
+            which, low = index >> 7, index & 127
+            value = jnp.zeros((fields, 128), F32)
+            for r in range(2 * blocks):
+                held = jnp.take_along_axis(grid_ref[:, r * 128 : (r + 1) * 128], low, axis=1)
+                value = jnp.where(which == r, held, value)
+            parts.append(value)
+        return jnp.concatenate(parts, axis=1)
+
+    general = jnp.concatenate([flag_ref[1:2, :]] * (size // 128), axis=1) > 0
+    for i in range(places):
+        m = places_by[i]
+        look_up(i, m)
+        by_lane = pick_by_lane(spots_of(1, i))
+        picked[:, part(1, m)] = jnp.where(general, other_ref[:, part(1, m)], by_lane)
+        for k in (0, 2):
+            spots = spots_of(k, i)
+            both = jnp.dot(u_ref[...], onehot(spots, PAIR), preferred_element_type=F32)
+            which = jnp.broadcast_to(spots >> 8, (fields, size))
+            top = jnp.zeros((fields, size), F32)
+            rest = jnp.zeros((fields, size), F32)
+            for r in range(blocks):
+                mine = which == r
+                top = jnp.where(mine, both[r * 16 : r * 16 + 8], top)
+                rest = jnp.where(mine, both[r * 16 + 8 : r * 16 + 16], rest)
+            picked[:, part(k, m)] = jnp.where(general, other_ref[:, part(k, m)], top + rest)
+        if i == 1:
+            pl.semaphore_wait(barrier, 3 * places - 1)
+        for n in range(0 if i == 1 else i, i + 1 if i else 0):
+            for k in others(n):
+                outward(k, places_by[n]).start()
+
+    for i in range(places):
+        for k in range(3):
+            sb_ref[:, part(k, places_by[i])] = onehot(spots_of(k, i), PAIR)
+            tb_ref[:, part(k, places_by[i])] = onehot(owned_of(k, places_by[i]), 128)
+    summed = jnp.zeros((heads * 16, 128), F32)
+    for i in reversed(range(places)):
+        m = places_by[i]
+        for k in others(i):
+            inward(k, m).wait_recv()
+        for k in range(3):
+            source = picked if (i, k) == (places - 1, 1) else inbox
+            both = halves(source[:, part(k, m)])
+            which = jnp.broadcast_to((owned_of(k, m) >> 7).astype(BF16), (16, size))
+            for h in range(heads):
+                ta_ref[h * 16 : (h + 1) * 16, k * size : (k + 1) * size] = jnp.where(which == jnp.bfloat16(h), both, zero)
+        right = jnp.concatenate([tb_ref[:, part(k, m)] for k in range(3)], axis=1)
+        summed = summed + lax.dot_general(
+            ta_ref[...], right, (((1,), (1,)), ((), ())), preferred_element_type=F32
+        )
+    totals = [summed[h * 16 : h * 16 + 8] + summed[h * 16 + 8 : h * 16 + 16] for h in range(heads)]
+    for i in range(places):
+        m = places_by[i]
+        for k in range(3):
+            owned = owned_of(k, m)
+            for j in range(size // 128):
+                index = jnp.broadcast_to(owned[:, j * 128 : (j + 1) * 128], (fields, 128))
+                low, which = index & 127, index >> 7
+                total = jnp.zeros((fields, 128), F32)
+                for h in range(heads):
+                    total = jnp.where(which == h, jnp.take_along_axis(totals[h], low, axis=1), total)
+                reply[:, pl.ds(pl.multiple_of((k * places + m) * size + j * 128, 128), 128)] = total
+        for k in others(i):
+            homeward(k, m).start()
+
+    for i in reversed(range(places)):
+        m = places_by[i]
+        for k in others(i):
+            returned(k, m).wait_recv()
+        for k in range(3):
+            source = reply if (i, k) == (places - 1, 1) else back
+            change = source[:, part(k, m)] - picked[:, part(k, m)]
+            change_ref[:, part(k, m)] = change
+            both = halves(change)
+            which = jnp.broadcast_to((spots_of(k, i) >> 8).astype(BF16), (16, size))
+            for r in range(blocks):
+                sa_ref[r * 16 : (r + 1) * 16, k * size : (k + 1) * size] = jnp.where(which == jnp.bfloat16(r), both, zero)
+        right = jnp.concatenate([sb_ref[:, part(k, m)] for k in range(3)], axis=1)
+        spread = lax.dot_general(sa_ref[...], right, (((1,), (1,)), ((), ())), preferred_element_type=F32)
         for r in range(blocks):
-            mine = which == r
-            top = jnp.where(mine, both[r * 16 : r * 16 + 8], top)
-            rest = jnp.where(mine, both[r * 16 + 8 : r * 16 + 16], rest)
-        picked[:, col] = jnp.where(general, other_ref[:, col], top + rest)
-
-    pl.semaphore_wait(barrier, known)
-    for k, d in peers:
-
-        @pl.when(reach[k, d])
-        def _():
-            copy(k, d, picked, inbox, l + d, l, out_sems, (g + k - 1, l + d)).start()
-
-    own = part(1, l)
-    inbox[:, own] = picked[:, own]
-    for k in (0, 2):
-        whole = slice(k * places * size, (k + 1) * places * size)
-
-        @pl.when(jnp.logical_not(heard[k, 0]))
-        def _():
-            inbox[:, whole] = jnp.zeros((fields, places * size), F32)
-
-        @pl.when(jnp.logical_not(reach[k, 0]))
-        def _():
-            back[:, whole] = jnp.zeros((fields, places * size), F32)
-
-    owned_low = iota((128, 128), 0).astype(BF16)
-    spot_low = iota((PAIR, 128), 0).astype(BF16)
-    for q in range(slots_all // 128):
-        col = slice(q * 128, (q + 1) * 128)
-        low = jnp.broadcast_to((owned_ref[q : q + 1, :] & 127).astype(BF16), (128, 128))
-        tb_ref[:, col] = jnp.where(low == owned_low, jnp.bfloat16(1), zero)
-        low = jnp.broadcast_to((spot_ref[q : q + 1, :] & (PAIR - 1)).astype(BF16), (PAIR, 128))
-        sb_ref[:, col] = jnp.where(low == spot_low, jnp.bfloat16(1), zero)
-
-    for k, d in reversed(peers):
-
-        @pl.when(heard[k, d])
-        def _():
-            copy(k, d, picked, inbox, l, l - d, out_sems, (g, l)).wait_recv()
-
-    for q in range(slots_all // 128):
-        col = slice(q * 128, (q + 1) * 128)
-        both = halves(inbox[:, col])
-        which = jnp.broadcast_to((owned_ref[q : q + 1, :] >> 7).astype(BF16), (16, 128))
-        for h in range(heads):
-            ta_ref[h * 16 : (h + 1) * 16, col] = jnp.where(which == jnp.bfloat16(h), both, zero)
-    summed = lax.dot_general(ta_ref[...], tb_ref[...], (((1,), (1,)), ((), ())), preferred_element_type=F32)
-    totals = [summed[h * 16 : h * 16 + 8] + summed[h * 16 + 8 : h * 16 + 16] for h in range(heads)]
-    for q in range(slots_all // 128):
-        col = slice(q * 128, (q + 1) * 128)
-        owned = jnp.broadcast_to(owned_ref[q : q + 1, :], (fields, 128))
-        low, which = owned & 127, owned >> 7
-        total = jnp.zeros((fields, 128), F32)
-        for h in range(heads):
-            total = jnp.where(which == h, jnp.take_along_axis(totals[h], low, axis=1), total)
-        reply[:, col] = total
-
-    for k, d in peers:
-
-        @pl.when(heard[k, d])
-        def _():
-            copy(k, d, reply, back, l - d, l, back_sems, (g - k + 1, l - d)).start()
-
-    back[:, own] = reply[:, own]
-    for k, d in reversed(peers):
-
-        @pl.when(reach[k, d])
-        def _():
-            copy(k, d, reply, back, l, l + d, back_sems, (g, l)).wait_recv()
-
-    for q in range(slots_all // 128):
-        col = slice(q * 128, (q + 1) * 128)
-        change = back[:, col] - picked[:, col]
-        change_ref[:, col] = change
-        both = halves(change)
-        which = jnp.broadcast_to((spot_ref[q : q + 1, :] >> 8).astype(BF16), (16, 128))
-        for r in range(blocks):
-            sa_ref[r * 16 : (r + 1) * 16, col] = jnp.where(which == jnp.bfloat16(r), both, zero)
-    spread = lax.dot_general(sa_ref[...], sb_ref[...], (((1,), (1,)), ((), ())), preferred_element_type=F32)
-    for r in range(blocks):
-        delta_ref[:, r * PAIR : (r + 1) * PAIR] = spread[r * 16 : r * 16 + 8] + spread[r * 16 + 8 : r * 16 + 16]
-
-    for k, d in peers:
-
-        @pl.when(reach[k, d])
-        def _():
-            copy(k, d, picked, inbox, l + d, l, out_sems, (g, l)).wait_send()
-
-        @pl.when(heard[k, d])
-        def _():
-            copy(k, d, reply, back, l - d, l, back_sems, (g, l)).wait_send()
+            col = slice(r * PAIR, (r + 1) * PAIR)
+            delta_ref[:, col] += spread[r * 16 : r * 16 + 8] + spread[r * 16 + 8 : r * 16 + 16]
+
+    for i in range(places):
+        for k in others(i):
+            outward(k, places_by[i]).wait_send()
+            homeward(k, places_by[i]).wait_send()
 
 
 SMEM = pl.BlockSpec(memory_space=pltpu.SMEM)
@@ -482,48 +502,48 @@
         pltpu.VMEM((span, 128), F32),
         pltpu.VMEM((table, 128), F32),
     ]
-    grid, order, live_nodes, flags, other = pl.pallas_call(
-        functools.partial(assemble_kernel, edge, slot_count),
+    order, live_nodes, flags, other, raw = pl.pallas_call(
+        functools.partial(order_kernel, edge, slot_count),
         out_shape=(
-            shape((fields, span), F32),
             shape((lines, 128), I32),
             shape((slot_rows, 128), I32),
             shape((8, 128), I32),
             shape((fields, slots_all), F32),
+            shape((fields, span), F32),
         ),
         in_specs=[HBM] * 6,
         out_specs=(VMEM,) * 5,
         scratch_shapes=[
-            pltpu.VMEM((fields, span), F32),
             pltpu.VMEM((32 * ROWS, 128), I32),
             pltpu.VMEM((slot_rows, 128), I32),
             pltpu.SMEM(counts.shape, I32),
             pltpu.SemaphoreType.DMA((4,)),
+            pltpu.VMEM((fields, span), F32),
         ]
         + general,
         compiler_params=pltpu.CompilerParams(vmem_limit_bytes=24 * 1024 * 1024),
-    )(element_values, map_rows, node_rows, counts, local_map, nodes)
-    delta, change = pl.pallas_call(
+    )(map_rows, node_rows, counts, element_values, local_map, nodes)
+    grid, delta, change = pl.pallas_call(
         functools.partial(exchange_kernel, groups, places, edge),
-        out_shape=(shape((fields, span), F32), shape((fields, slots_all), F32)),
+        out_shape=(shape((fields, span), F32), shape((fields, span), F32), shape((fields, slots_all), F32)),
         in_specs=[VMEM] * 6,
-        out_specs=(VMEM, VMEM),
+        out_specs=(VMEM,) * 3,
         scratch_shapes=[pltpu.VMEM((fields, slots_all), F32)] * 4
         + [
-            pltpu.VMEM((slot_rows, 128), I32),
+            pltpu.VMEM((places * ((3 * slot_count // 128 + 7) // 8 * 8), 128), I32),
             pltpu.VMEM((2 * tall16, span), BF16),
             pltpu.VMEM((128, span), BF16),
             pltpu.VMEM((lines // 2 * 16, PAIR), BF16),
-            pltpu.VMEM((owned // 128 * 16, slots_all), BF16),
+            pltpu.VMEM((owned // 128 * 16, 3 * slot_count), BF16),
             pltpu.VMEM((128, slots_all), BF16),
-            pltpu.VMEM((lines // 2 * 16, slots_all), BF16),
+            pltpu.VMEM((lines // 2 * 16, 3 * slot_count), BF16),
             pltpu.VMEM((PAIR, slots_all), BF16),
         ]
-        + [pltpu.SemaphoreType.DMA((3 * (2 * places - 1),))] * 4,
+        + [pltpu.SemaphoreType.DMA((3 * places,))] * 4,
         compiler_params=pltpu.CompilerParams(
             collective_id=0, has_side_effects=True, vmem_limit_bytes=40 * 1024 * 1024
         ),
-    )(order, grid, live_nodes, owned_rows, flags, other)
+    )(order, live_nodes, owned_rows, flags, other, raw)
     return pl.pallas_call(
         functools.partial(finish_kernel, edge, slot_count),
         out_shape=shape((fields, span), F32),

time: 23.8 us -> 22 us (0.924); the launches traced: 23.7 us -> 21.6 us
  Pallas kernels: 23.7 us -> 21.6 us
    pallas_call x1, Pallas kernels: 20.5 us -> 18.7 us  [on_device(): pl.pallas_call(functools.partial(exchange_kernel, groups, places, edge),...]
    pallas_call x1, Pallas kernels: 1.8 us -> 1.51 us  [on_device(): pl.pallas_call(functools.partial(order_kernel, edge, slot_count), out_sha...]
where the time goes in v3:
time: 22 us; the launch traced here: 21.6 us
  Pallas kernels  21.6 us (98%)
    pallas_call x1, Pallas kernels, on_device(): pl.pallas_call(functools.partial(exchange_kernel, groups, places, edge),...  18.7 us
    pallas_call x1, Pallas kernels, on_device(): pl.pallas_call(functools.partial(order_kernel, edge, slot_count), out_sha...  1.51 us
    pallas_call x1, Pallas kernels, on_device(): pl.pallas_call(functools.partial(finish_kernel, edge, slot_count), out_sh...  1.37 us

profile of v3, /device:TPU:1, one launch (start us, length us, event | category | flops | bytes accessed | tf_op | source)
XLA Modules:
  0.0 21.6 jit_solution(7222999192076094724)
XLA Ops:
  0.0 0.0 copy-start
  0.0 1.5 %shard_map.55 = (s32[108,128]{1,0:T(8,128)S(1)}, s32[24,128]{1,0:T(8,128)S(1)}, s32[8,128]{1,0:T(8,128)S(1)}, f32[8,3072]{1,0:T(8,128)S(1)}, f32[8,13824]{1,0:T(8,128)S(1)}) custom-call(s32[108,128]{1,0:T(8,128)} %bitcast.6, s32[24,128]{1,0:T(8,128)} %bitcast.7, s32[12]{0:T(128)} %bitcast.10, f32[8,13824]{1,0:T(8,128)} %value_hbm.3, s32[13824]{0:T(1024)} %map_flat.3, ...), custom_call_target="tpu_custom_call" | custom-call | tf_op jit(solution)/shard_map/pallas_call | solution.py:505
  1.5 0.0 copy-done
  1.5 18.7 %shard_map.56 = (f32[8,13824]{1,0:T(8,128)S(1)}, f32[8,13824]{1,0:T(8,128)S(1)}, f32[8,3072]{1,0:T(8,128)S(1)}) custom-call(s32[108,128]{1,0:T(8,128)S(1)} %get-tuple-element.13.order_ref, s32[24,128]{1,0:T(8,128)S(1)} %get-tuple-element.14.node_ref, s32[24,128]{1,0:T(8,128)S(1)} %bitcast.5, s32[8,128]{1,0:T(8,128)S(1)} %get-tuple-element.15.flag_ref, ...), custom_call_target="tpu_custom_call" | custom-call | tf_op jit(solution)/shard_map/pallas_call | solution.py:526
  20.2 1.4 %shard_map.57 = f32[8,13824]{1,0:T(8,128)} custom-call(f32[8,13824]{1,0:T(8,128)S(1)} %get-tuple-element.18.delta_in, f32[8,13824]{1,0:T(8,128)S(1)} %get-tuple-element.19.grid_ref, s32[8,128]{1,0:T(8,128)S(1)} %get-tuple-element.15.flag_ref, f32[8,3072]{1,0:T(8,128)S(1)} %get-tuple-element.20.change_ref, s32[12]{0:T(128)} %bitcast.11, ...), custom_call_target="tpu_custom_call" | custom-call | tf_op jit(solution)/shard_map/pallas_call | solution.py:547
Async XLA Ops:
  0.0 1.5 %copy-start = (s32[1,3072]{1,0:T(1,128)S(1)}, s32[1,3072]{1,0:T(1,128)}, u32[]{:S(2)}) copy-start(s32[1,3072]{1,0:T(1,128)} %param.9) | copy-start | bytes 36868

commit v4 on v3

--- a/solution.py
+++ b/solution.py
@@ -197,7 +197,6 @@
         grid_ref[:, s * NODES : (s + 1) * NODES] = value_ref[:, pl.ds(pl.multiple_of(e * NODES, NODES), NODES)]
         for r in range(ROWS):
             order_ref[s * ROWS + r : s * ROWS + r + 1, :] = lab_ref[pl.ds(e * ROWS + r, 1), :]
-    bad = jnp.sum(count_mismatches(order_ref, edge)) + jnp.sum(wrong)
     nodes.wait()
     counts.wait()
     per = slot_count // 128
@@ -207,6 +206,7 @@
         limit = jnp.where(row_of // per == p, count_ref[p], limit)
     live = (row_of % per) * 128 + iota((slot_rows, 128), 1) < limit
     node_ref[...] = jnp.where(live, raw_ref[...], -1)
+    bad = jnp.sum(count_mismatches(order_ref, edge)) + jnp.sum(wrong)
     flag_ref[1:2, :] = jnp.full((1, 128), bad, I32)
 
     @pl.when(bad > 0)
@@ -294,12 +294,12 @@
 def exchange_kernel(
     groups, places, edge, order_ref, node_ref, owned_ref, flag_ref, other_ref, raw_ref,
     grid_ref, delta_ref, change_ref,
-    picked, inbox, reply, back, spot_ref, pa_ref, pb_ref, u_ref, ta_ref, tb_ref, sa_ref, sb_ref,
+    picked, inbox, reply, back, spot_ref, pa_ref, pb_ref, u_ref, tb_ref, sb_ref,
     send_out, recv_out, send_back, recv_back,
 ):
     fields, slots_all = change_ref.shape
     size = slots_all // (3 * places)
-    heads = ta_ref.shape[0] // 16
+    heads = 2 * size // 128
     blocks = grid_ref.shape[1] // PAIR
     g, l = lax.axis_index("grp"), lax.axis_index("loc")
 
@@ -355,7 +355,6 @@
     sweep(grid_ref, edge)
     for r in range(blocks):
         u_ref[r * 16 : (r + 1) * 16, :] = halves(grid_ref[:, r * PAIR : (r + 1) * PAIR])
-    delta_ref[...] = jnp.zeros(delta_ref.shape, F32)
 
     def spots_of(k, i):
         row = i * (spot_ref.shape[0] // places) + k * (size // 128)
@@ -418,22 +417,23 @@
 
     for i in range(places):
         for k in range(3):
-            sb_ref[:, part(k, places_by[i])] = onehot(spots_of(k, i), PAIR)
+            column = ((places - 1 - i) * 3 + k) * size
+            sb_ref[:, column : column + size] = onehot(spots_of(k, i), PAIR)
             tb_ref[:, part(k, places_by[i])] = onehot(owned_of(k, places_by[i]), 128)
     summed = jnp.zeros((heads * 16, 128), F32)
     for i in reversed(range(places)):
         m = places_by[i]
         for k in others(i):
             inward(k, m).wait_recv()
+        lefts = []
         for k in range(3):
             source = picked if (i, k) == (places - 1, 1) else inbox
             both = halves(source[:, part(k, m)])
             which = jnp.broadcast_to((owned_of(k, m) >> 7).astype(BF16), (16, size))
-            for h in range(heads):
-                ta_ref[h * 16 : (h + 1) * 16, k * size : (k + 1) * size] = jnp.where(which == jnp.bfloat16(h), both, zero)
+            lefts.append(jnp.concatenate([jnp.where(which == jnp.bfloat16(h), both, zero) for h in range(heads)], axis=0))
         right = jnp.concatenate([tb_ref[:, part(k, m)] for k in range(3)], axis=1)
         summed = summed + lax.dot_general(
-            ta_ref[...], right, (((1,), (1,)), ((), ())), preferred_element_type=F32
+            jnp.concatenate(lefts, axis=1), right, (((1,), (1,)), ((), ())), preferred_element_type=F32
         )
     totals = [summed[h * 16 : h * 16 + 8] + summed[h * 16 + 8 : h * 16 + 16] for h in range(heads)]
     for i in range(places):
@@ -450,23 +450,33 @@
         for k in others(i):
             homeward(k, m).start()
 
-    for i in reversed(range(places)):
-        m = places_by[i]
-        for k in others(i):
-            returned(k, m).wait_recv()
-        for k in range(3):
-            source = reply if (i, k) == (places - 1, 1) else back
-            change = source[:, part(k, m)] - picked[:, part(k, m)]
-            change_ref[:, part(k, m)] = change
-            both = halves(change)
-            which = jnp.broadcast_to((spots_of(k, i) >> 8).astype(BF16), (16, size))
-            for r in range(blocks):
-                sa_ref[r * 16 : (r + 1) * 16, k * size : (k + 1) * size] = jnp.where(which == jnp.bfloat16(r), both, zero)
-        right = jnp.concatenate([sb_ref[:, part(k, m)] for k in range(3)], axis=1)
-        spread = lax.dot_general(sa_ref[...], right, (((1,), (1,)), ((), ())), preferred_element_type=F32)
+    order = [i for i in reversed(range(places))]
+    for first, last in tuple((n, n + 1) for n in range(places)):
+        together = order[first:last]
+        lefts = []
+        for i in together:
+            m = places_by[i]
+            for k in others(i):
+                returned(k, m).wait_recv()
+            for k in range(3):
+                source = reply if (i, k) == (places - 1, 1) else back
+                change = source[:, part(k, m)] - picked[:, part(k, m)]
+                change_ref[:, part(k, m)] = change
+                both = halves(change)
+                which = jnp.broadcast_to((spots_of(k, i) >> 8).astype(BF16), (16, size))
+                lefts.append(jnp.concatenate([jnp.where(which == jnp.bfloat16(r), both, zero) for r in range(blocks)], axis=0))
+        depth = len(together) * 3 * size
+        start = first * 3 * size
+        spread = lax.dot_general(
+            jnp.concatenate(lefts, axis=1), sb_ref[:, start : start + depth], (((1,), (1,)), ((), ())), preferred_element_type=F32
+        )
         for r in range(blocks):
             col = slice(r * PAIR, (r + 1) * PAIR)
-            delta_ref[:, col] += spread[r * 16 : r * 16 + 8] + spread[r * 16 + 8 : r * 16 + 16]
+            moved = spread[r * 16 : r * 16 + 8] + spread[r * 16 + 8 : r * 16 + 16]
+            if first == 0:
+                delta_ref[:, col] = moved
+            else:
+                delta_ref[:, col] += moved
 
     for i in range(places):
         for k in others(i):
@@ -483,7 +493,6 @@
     fields, span = element_values.shape
     slots_all = send_node.shape[1]
     slot_count = slots_all // (3 * places)
-    owned = 2 * slot_count
     edge = blocks_along(span)
     local = ((SIDE - 1) * edge + 1) ** 3
     tall16 = (local + 2047) // 2048 * 16
@@ -534,9 +543,7 @@
             pltpu.VMEM((2 * tall16, span), BF16),
             pltpu.VMEM((128, span), BF16),
             pltpu.VMEM((lines // 2 * 16, PAIR), BF16),
-            pltpu.VMEM((owned // 128 * 16, 3 * slot_count), BF16),
             pltpu.VMEM((128, slots_all), BF16),
-            pltpu.VMEM((lines // 2 * 16, 3 * slot_count), BF16),
             pltpu.VMEM((PAIR, slots_all), BF16),
         ]
         + [pltpu.SemaphoreType.DMA((3 * places,))] * 4,

time: 22 us -> 22 us (level)
  no operation moved by 1% of the time
where the time goes in v4:
time: 22 us; the launch traced here: 21.6 us
  Pallas kernels  21.5 us (98%)
    pallas_call x1, Pallas kernels, on_device(): pl.pallas_call(functools.partial(exchange_kernel, groups, places, edge),...  18.7 us
    pallas_call x1, Pallas kernels, on_device(): pl.pallas_call(functools.partial(order_kernel, edge, slot_count), out_sha...  1.52 us
    pallas_call x1, Pallas kernels, on_device(): pl.pallas_call(functools.partial(finish_kernel, edge, slot_count), out_sh...  1.37 us

profile of v4, /device:TPU:1, one launch (start us, length us, event | category | flops | bytes accessed | tf_op | source)
XLA Modules:
  0.0 21.6 jit_solution(199550604046336628)
XLA Ops:
  0.0 0.0 copy-start
  0.0 1.5 %shard_map.55 = (s32[108,128]{1,0:T(8,128)S(1)}, s32[24,128]{1,0:T(8,128)S(1)}, s32[8,128]{1,0:T(8,128)S(1)}, f32[8,3072]{1,0:T(8,128)S(1)}, f32[8,13824]{1,0:T(8,128)S(1)}) custom-call(s32[108,128]{1,0:T(8,128)} %bitcast.6, s32[24,128]{1,0:T(8,128)} %bitcast.7, s32[12]{0:T(128)} %bitcast.10, f32[8,13824]{1,0:T(8,128)} %value_hbm.3, s32[13824]{0:T(1024)} %map_flat.3, ...), custom_call_target="tpu_custom_call" | custom-call | tf_op jit(solution)/shard_map/pallas_call | solution.py:514
  1.5 0.0 copy-done
  1.5 18.7 %shard_map.56 = (f32[8,13824]{1,0:T(8,128)S(1)}, f32[8,13824]{1,0:T(8,128)S(1)}, f32[8,3072]{1,0:T(8,128)S(1)}) custom-call(s32[108,128]{1,0:T(8,128)S(1)} %get-tuple-element.13.order_ref, s32[24,128]{1,0:T(8,128)S(1)} %get-tuple-element.14.node_ref, s32[24,128]{1,0:T(8,128)S(1)} %bitcast.5, s32[8,128]{1,0:T(8,128)S(1)} %get-tuple-element.15.flag_ref, ...), custom_call_target="tpu_custom_call" | custom-call | tf_op jit(solution)/shard_map/pallas_call | solution.py:535
  20.2 1.4 %shard_map.57 = f32[8,13824]{1,0:T(8,128)} custom-call(f32[8,13824]{1,0:T(8,128)S(1)} %get-tuple-element.18.delta_in, f32[8,13824]{1,0:T(8,128)S(1)} %get-tuple-element.19.grid_ref, s32[8,128]{1,0:T(8,128)S(1)} %get-tuple-element.15.flag_ref, f32[8,3072]{1,0:T(8,128)S(1)} %get-tuple-element.20.change_ref, s32[12]{0:T(128)} %bitcast.11, ...), custom_call_target="tpu_custom_call" | custom-call | tf_op jit(solution)/shard_map/pallas_call | solution.py:554
Async XLA Ops:
  0.0 1.5 %copy-start = (s32[1,3072]{1,0:T(1,128)S(1)}, s32[1,3072]{1,0:T(1,128)}, u32[]{:S(2)}) copy-start(s32[1,3072]{1,0:T(1,128)} %param.9) | copy-start | bytes 36868

commit v5 on v4

--- a/solution.py
+++ b/solution.py
@@ -467,8 +467,16 @@
                 lefts.append(jnp.concatenate([jnp.where(which == jnp.bfloat16(r), both, zero) for r in range(blocks)], axis=0))
         depth = len(together) * 3 * size
         start = first * 3 * size
-        spread = lax.dot_general(
-            jnp.concatenate(lefts, axis=1), sb_ref[:, start : start + depth], (((1,), (1,)), ((), ())), preferred_element_type=F32
+        left = jnp.concatenate(lefts, axis=1)
+        cut = blocks // 2 * 16
+        spread = jnp.concatenate(
+            [
+                lax.dot_general(
+                    part, sb_ref[:, start : start + depth], (((1,), (1,)), ((), ())), preferred_element_type=F32
+                )
+                for part in (left[:cut], left[cut:])
+            ],
+            axis=0,
         )
         for r in range(blocks):
             col = slice(r * PAIR, (r + 1) * PAIR)

time: 22 us -> 21.2 us (0.964)
  the two profiles are of different devices: /device:TPU:1 before, /device:TPU:0 now
where the time goes in v5:
time: 21.2 us; the launch traced here: 21.1 us
  Pallas kernels  21 us (99%)
    pallas_call x1, Pallas kernels, on_device(): pl.pallas_call(functools.partial(exchange_kernel, groups, places, edge),...  18.1 us
    pallas_call x1, Pallas kernels, on_device(): pl.pallas_call(functools.partial(order_kernel, edge, slot_count), out_sha...  1.52 us
    pallas_call x1, Pallas kernels, on_device(): pl.pallas_call(functools.partial(finish_kernel, edge, slot_count), out_sh...  1.37 us

profile of v5, /device:TPU:0, one launch (start us, length us, event | category | flops | bytes accessed | tf_op | source)
XLA Modules:
  0.0 21.1 jit_solution(5832983793897484622)
XLA Ops:
  0.0 0.0 copy-start
  0.0 1.5 %shard_map.55 = (s32[108,128]{1,0:T(8,128)S(1)}, s32[24,128]{1,0:T(8,128)S(1)}, s32[8,128]{1,0:T(8,128)S(1)}, f32[8,3072]{1,0:T(8,128)S(1)}, f32[8,13824]{1,0:T(8,128)S(1)}) custom-call(s32[108,128]{1,0:T(8,128)} %bitcast.6, s32[24,128]{1,0:T(8,128)} %bitcast.7, s32[12]{0:T(128)} %bitcast.10, f32[8,13824]{1,0:T(8,128)} %value_hbm.3, s32[13824]{0:T(1024)} %map_flat.3, ...), custom_call_target="tpu_custom_call" | custom-call | tf_op jit(solution)/shard_map/pallas_call | solution.py:522
  1.5 0.0 copy-done
  1.5 18.1 %shard_map.56 = (f32[8,13824]{1,0:T(8,128)S(1)}, f32[8,13824]{1,0:T(8,128)S(1)}, f32[8,3072]{1,0:T(8,128)S(1)}) custom-call(s32[108,128]{1,0:T(8,128)S(1)} %get-tuple-element.13.order_ref, s32[24,128]{1,0:T(8,128)S(1)} %get-tuple-element.14.node_ref, s32[24,128]{1,0:T(8,128)S(1)} %bitcast.5, s32[8,128]{1,0:T(8,128)S(1)} %get-tuple-element.15.flag_ref, ...), custom_call_target="tpu_custom_call" | custom-call | tf_op jit(solution)/shard_map/pallas_call | solution.py:543
  19.7 1.4 %shard_map.57 = f32[8,13824]{1,0:T(8,128)} custom-call(f32[8,13824]{1,0:T(8,128)S(1)} %get-tuple-element.18.delta_in, f32[8,13824]{1,0:T(8,128)S(1)} %get-tuple-element.19.grid_ref, s32[8,128]{1,0:T(8,128)S(1)} %get-tuple-element.15.flag_ref, f32[8,3072]{1,0:T(8,128)S(1)} %get-tuple-element.20.change_ref, s32[12]{0:T(128)} %bitcast.11, ...), custom_call_target="tpu_custom_call" | custom-call | tf_op jit(solution)/shard_map/pallas_call | solution.py:562
Async XLA Ops:
  0.0 1.5 %copy-start = (s32[1,3072]{1,0:T(1,128)S(1)}, s32[1,3072]{1,0:T(1,128)}, u32[]{:S(2)}) copy-start(s32[1,3072]{1,0:T(1,128)} %param.9) | copy-start | bytes 36868
